TPU v7x, 128 devices: a whole 4x4x4 slice. The times are simulated.
128 devices in a mesh: slab: 16 (over z, x), tile: 8 (over y, core).
Axes of the slice: x: 4, y: 4, z: 4, core: 2. Of those that a mesh axis runs over, the one named last changes fastest.
Arguments:
- fixed_planes: float32 [512, 512, 128], P(('slab', 'tile')), may hold values from -6 to 6
- moving_planes: float32 [2, 512, 512, 128], P(None, ('slab', 'tile')), may hold values from -6 to 6
- pair_dest: int32 [2, 512], P(None, ('slab', 'tile')), may hold values from 0 to 15, as said below
- pair_slot: int32 [2, 512], P(None, ('slab', 'tile')), may hold values from 0 to 3, as said below
- plane_shift: int32 [2, 2, 512], P(None, None, ('slab', 'tile')), may hold values from -24 to 24
- live_count: int32 [128], P(('slab', 'tile')), may hold values from 1 to 4, 298 in all
- piece_block: int32 [8192], P(('slab', 'tile')), may hold values from 0 to 2047, as said below
Outputs:
- peaks: float32 [2, 512], P(None, ('slab', 'tile'))
- blocks: float32 [2048, 32, 128], P(('slab', 'tile'))
Inputs may be any that keep to these rules, and one draw needn't show every extreme that they name: `pair_dest`: round 0 entries lie in 0 to 15 and round 1 entries in 0 to 7. With pair_slot, every fixed plane of every device is targeted by exactly one moving plane in each round. In round 0 no device targets more than 2 planes of any one device, in round 1 no more than 2; in every round every device targets exactly that many planes of some device. `pair_slot`: drawn together with pair_dest. `live_count`: the counts sum to 298 and some device has 4. `piece_block`: block b is owned by device b // 16 along slab+tile. At most 2 pieces of one device go to blocks of one owner, and the first 2 pieces of every device go to blocks of one owner.
All inputs are finite; a program needn't handle non-finite values.
Results may differ from a plain program's by a relative error of at most 0.0003.
Values sent between devices are 32-bit elements; how exact they have to be, the bound alone decides.
A program may use at most 128 MiB of HBM per device.

v0:
```python
import math

import jax
import jax.numpy as jnp
from jax import lax
from jax.sharding import PartitionSpec as P

PIECES = 16
OWNED = 16


FLOOR = 0.25
CENTER = 4.0
HIGHEST = lax.Precision.HIGHEST


def in_blocks(x, dim, length):
    before, after = (x.shape[:dim], x.shape[dim + 1 :])
    return jnp.moveaxis(x.reshape(*before, length, -1, *after), dim, 0)


def joined_along(blocks, dim):
    dims = list(blocks.shape[1:])
    dims[dim] *= blocks.shape[0]
    return jnp.moveaxis(blocks, 0, dim).reshape(dims)


def one_exchange(x, axis, axes, splits, concats):
    sizes = [lax.axis_size(a) for a in axes]
    blocks = in_blocks(x, splits[0], sizes[0])
    blocks = jnp.moveaxis(in_blocks(blocks, splits[1] + 1, sizes[1]), 0, 1)
    inside = blocks.shape[2:]
    blocks = blocks.reshape(-1, *inside)
    blocks = lax.all_to_all(blocks, axis, split_axis=0, concat_axis=0, tiled=True)
    blocks = joined_along(blocks.reshape(*sizes, *inside), concats[0] + 1)
    return joined_along(blocks, concats[1])


def tables(length):
    index = lax.iota(jnp.int32, length)
    angle = (index[:, None] * index[None, :] % length).astype(jnp.float32) * (
        2.0 * math.pi / length
    )
    factor = 1.0 / math.sqrt(length)
    return (jnp.cos(angle) * factor, jnp.sin(angle) * factor)


def forward(planes, row_tables, column_tables):
    height, breadth = (planes.shape[1], planes.shape[2])
    stacked = jnp.concatenate([row_tables[0], -row_tables[1]], 0)
    halves = jnp.einsum("rk,bkc->brc", stacked, planes, precision=HIGHEST)
    mixed = jnp.einsum(
        "brc,cd->brd",
        halves,
        jnp.concatenate([column_tables[0], column_tables[1]], 1),
        precision=HIGHEST,
    )
    real_part = mixed[:, :height, :breadth] + mixed[:, height:, breadth:]
    imag_part = mixed[:, height:, :breadth] - mixed[:, :height, breadth:]
    return (real_part, imag_part)


def inverse(real_part, imag_part, row_tables, column_tables):
    height, breadth = (real_part.shape[1], real_part.shape[2])
    joined = jnp.concatenate([real_part, imag_part], 1)
    mixed = jnp.einsum(
        "brc,cd->brd",
        joined,
        jnp.concatenate([column_tables[0], column_tables[1]], 1),
        precision=HIGHEST,
    )
    first_real = mixed[:, :height, :breadth] - mixed[:, height:, breadth:]
    first_imag = mixed[:, :height, breadth:] + mixed[:, height:, :breadth]
    stacked = jnp.concatenate([row_tables[0], -row_tables[1]], 1)
    return jnp.einsum(
        "rk,bkc->brc", stacked, jnp.concatenate([first_real, first_imag], 1), precision=HIGHEST
    )


def pack(values, target, labels, usable, peers, capacity):
    item_count = target.shape[0]
    peer_ids = lax.iota(jnp.int32, peers)
    hits = ((target[:, None] == peer_ids[None, :]) & usable[:, None]).astype(jnp.int32)
    rank = jnp.sum((jnp.cumsum(hits, 0) - hits) * hits, 1)
    position = jnp.where(usable, target * capacity + rank, -1)
    slot_ids = lax.iota(jnp.int32, peers * capacity)
    chosen = (position[None, :] == slot_ids[:, None]).astype(jnp.int32)
    filled = jnp.sum(chosen, 1) > 0
    source = jnp.sum(chosen * lax.iota(jnp.int32, item_count)[None, :], 1)
    gathered = jnp.take(values, source, 0)
    packed = jnp.where(filled.reshape((-1,) + (1,) * (values.ndim - 1)), gathered, 0.0)
    packed_labels = jnp.where(filled, jnp.take(labels, source, 0), -1)
    return (
        packed.reshape((peers, capacity) + values.shape[1:]),
        packed_labels.reshape(peers, capacity),
    )


def arrange(received, labels, wanted):
    flat = received.reshape((-1,) + received.shape[2:])
    flat_labels = labels.reshape(-1)
    match = (flat_labels[None, :] == lax.iota(jnp.int32, wanted)[:, None]).astype(jnp.int32)
    anchor = jnp.sum(match * lax.iota(jnp.int32, flat_labels.shape[0])[None, :], 1)
    return jnp.take(flat, anchor, 0)


def shift_planes(planes, downward, sideways):
    return jax.vmap(
        lambda plane, first_shift, second_shift: jnp.roll(
            plane, (first_shift, second_shift), axis=(0, 1)
        )
    )(planes, downward, sideways)


def local(fixed_planes, moving_planes, pair_dest, pair_slot, plane_shift, live_count, piece_block):
    planes_here, height, breadth = fixed_planes.shape
    row_tables = tables(height)
    column_tables = tables(breadth)
    fixed_real, fixed_imag = forward(fixed_planes, row_tables, column_tables)
    everyone = jnp.ones((planes_here,), bool)
    slab_peers = lax.axis_size("slab")
    tile_peers = lax.axis_size("tile")
    slab_capacity = max(2, (planes_here + slab_peers - 1) // slab_peers)
    tile_capacity = max(2, (planes_here + tile_peers - 1) // tile_peers)
    first_send, first_labels = pack(
        moving_planes[0], pair_dest[0], pair_slot[0], everyone, slab_peers, slab_capacity
    )
    first_got, first_got_labels = (
        lax.all_to_all(first_send, "slab", split_axis=0, concat_axis=0, tiled=True),
        lax.all_to_all(first_labels, "slab", split_axis=0, concat_axis=0, tiled=True),
    )
    first_partner = arrange(first_got, first_got_labels, planes_here)
    second_send, second_labels = pack(
        moving_planes[1], pair_dest[1], pair_slot[1], everyone, tile_peers, tile_capacity
    )
    second_got, second_got_labels = (
        lax.all_to_all(second_send, "tile", split_axis=0, concat_axis=0, tiled=True),
        lax.all_to_all(second_labels, "tile", split_axis=0, concat_axis=0, tiled=True),
    )
    second_partner = arrange(second_got, second_got_labels, planes_here)
    is_live = lax.iota(jnp.int32, planes_here) < live_count[0]
    weighted_sum = fixed_planes
    weight_total = jnp.ones((planes_here,), jnp.float32)
    peak_list = []
    for round_index, partner in enumerate((first_partner, second_partner)):
        moving_real, moving_imag = forward(partner, row_tables, column_tables)
        cross_real = fixed_real * moving_real + fixed_imag * moving_imag
        cross_imag = fixed_imag * moving_real - fixed_real * moving_imag
        magnitude = jnp.sqrt(cross_real * cross_real + cross_imag * cross_imag + FLOOR**2)
        surface = inverse(cross_real / magnitude, cross_imag / magnitude, row_tables, column_tables)
        peak_value = jnp.max(surface, axis=(1, 2))
        weight = jax.nn.sigmoid(peak_value - CENTER)
        moved = shift_planes(partner, plane_shift[round_index, 0], plane_shift[round_index, 1])
        weighted_sum = weighted_sum + weight[:, None, None] * moved
        weight_total = weight_total + weight
        peak_list.append(jnp.where(is_live, peak_value, 0.0))
    merged = weighted_sum / weight_total[:, None, None]
    band_rows = height // PIECES
    pieces = merged.reshape(planes_here * PIECES, band_rows, breadth)
    piece_live = lax.iota(jnp.int32, planes_here * PIECES) // PIECES < live_count[0]
    owners = piece_block // OWNED
    within = piece_block % OWNED
    all_peers = slab_peers * tile_peers
    route_capacity = max(2, (planes_here * PIECES + all_peers - 1) // all_peers)
    packed, packed_labels = pack(pieces, owners, within, piece_live, all_peers, route_capacity)
    shaped = packed.reshape((slab_peers, tile_peers) + packed.shape[1:])
    shaped_labels = packed_labels.reshape(slab_peers, tile_peers, route_capacity)
    arrived, arrived_labels = (
        one_exchange(shaped, ("slab", "tile"), ("slab", "tile"), (0, 1), (0, 1)),
        one_exchange(shaped_labels, ("slab", "tile"), ("slab", "tile"), (0, 1), (0, 1)),
    )
    flat = arrived.reshape(-1, band_rows * breadth)
    flat_labels = arrived_labels.reshape(-1)
    selector = (flat_labels[None, :] == lax.iota(jnp.int32, OWNED)[:, None]).astype(jnp.float32)
    blocks = jnp.dot(selector, flat, precision=HIGHEST).reshape(OWNED, band_rows, breadth)
    return (jnp.stack(peak_list), blocks)


def solution(mesh):
    placed = (
        P(("slab", "tile"), None, None),
        P(None, ("slab", "tile"), None, None),
        P(None, ("slab", "tile")),
        P(None, ("slab", "tile")),
        P(None, None, ("slab", "tile")),
        P(("slab", "tile")),
        P(("slab", "tile")),
    )
    return jax.shard_map(
        local,
        mesh=mesh,
        in_specs=placed,
        out_specs=(P(None, ("slab", "tile")), P(("slab", "tile"), None, None)),
        check_vma=False,
    )
```

profile of v0, /device:TPU:1, one launch (start us, length us, event | category | flops | bytes accessed | tf_op | source)
XLA Modules:
  0.0 377.5 jit_solution(9470496080900363065)
XLA Ops:
  4.7 6.0 %all-to-all-start.2 = ((s32[8,1,2]{2,1,0:T(1,128)}), s32[8,1,2]{2,1,0:T(1,128)S(1)}, u32[]{:S(2)}, u32[]{:S(2)}) async-start(s32[8,1,2]{2,1,0:T(1,128)} %bitcast.28), calls=%async_computation.2 | async-start | bytes 8192 | tf_op jit(solution)/shard_map/all_to_all | solution.py:138
  21.3 7.6 %all-to-all-start = ((s32[16,1,2]{2,1,0:T(1,128)}), s32[16,1,2]{2,1,0:T(1,128)S(1)}, u32[]{:S(2)}, u32[]{:S(2)}) async-start(s32[16,1,2]{2,1,0:T(1,128)} %bitcast.13), calls=%async_computation | async-start | bytes 16384 | tf_op jit(solution)/shard_map/all_to_all | solution.py:130
  28.9 4.7 %select_select_fusion.2 = f32[8,2,512,128]{3,2,1,0:T(8,128)} fusion(f32[8,2,512,128]{3,2,1,0:T(8,128)} %bitcast.158, pred[8,2]{1,0:T(8,128)(4,1)S(1)} %compare_and_fusion.2, pred[8,2]{1,0:T(8,128)(4,1)S(1)} %gt.89), kind=kLoop, calls=%fused_computation.14 | loop fusion | flops 2097152 | bytes 8388640 | tf_op jit(solution)/shard_map/jit(_where)/select_n | solution.py:91
  35.3 6.2 %all-to-all-start.3 = ((f32[8,2,512,128]{3,2,1,0:T(8,128)}), f32[8,2,512,128]{3,2,1,0:T(8,128)}, u32[]{:S(2)}, u32[]{:S(2)}) async-start(f32[8,2,512,128]{3,2,1,0:T(8,128)} %select_select_fusion.2), calls=%async_computation.3 | async-start | bytes 8388608 | tf_op jit(solution)/shard_map/all_to_all | solution.py:137
  41.7 4.3 %gather_fusion = f32[32,512,128]{2,1,0:T(8,128)} fusion(f32[4,512,128]{2,1,0:T(8,128)S(1)} %get-tuple-element.35, s32[1024]{0:T(1024)S(1)} %pad_clamp_fusion.4), kind=kCustom, calls=%fused_computation.4 | custom fusion | bytes 16777344 | tf_op jit(solution)/shard_map/jit(_take)/gather | solution.py:90
  46.0 8.4 %select_select_fusion = f32[16,2,512,128]{3,2,1,0:T(8,128)} fusion(f32[16,2,512,128]{3,2,1,0:T(8,128)} %bitcast.156, pred[16,2]{1,0:T(8,128)(4,1)S(1)} %compare_and_fusion.1, pred[16,2]{1,0:T(8,128)(4,1)S(1)} %gt.85), kind=kLoop, calls=%fused_computation.11 | loop fusion | flops 4194304 | bytes 16777280 | tf_op jit(solution)/shard_map/jit(_where)/select_n | solution.py:91
  54.4 35.9 %all-to-all-done.3 = f32[8,2,512,128]{3,2,1,0:T(8,128)} async-done(((f32[8,2,512,128]{3,2,1,0:T(8,128)}), f32[8,2,512,128]{3,2,1,0:T(8,128)}, u32[]{:S(2)}, u32[]{:S(2)}) %all-to-all-start.3) | async-done | bytes 4194336 | tf_op jit(solution)/shard_map/all_to_all | solution.py:137
  90.3 5.0 %all-to-all-start.1 = ((f32[16,2,512,128]{3,2,1,0:T(8,128)}), f32[16,2,512,128]{3,2,1,0:T(8,128)}, u32[]{:S(2)}, u32[]{:S(2)}) async-start(f32[16,2,512,128]{3,2,1,0:T(8,128)} %select_select_fusion), calls=%async_computation.1 | async-start | bytes 16777216 | tf_op jit(solution)/shard_map/all_to_all | solution.py:129
  99.5 4.2 %multiply_negate_fusion = (f32[512,512]{1,0:T(8,128)S(1)}, f32[512,512]{1,0:T(8,128)S(1)}) fusion(), kind=kLoop, calls=%fused_computation.77 | loop fusion | flops 4456448 | bytes 2097152 | tf_op jit(solution)/shard_map/neg | solution.py:50
  108.0 5.3 %fusion.20 = f32[4,1024,256]{2,1,0:T(8,128)} fusion(f32[1024,4,128]{2,0,1:T(8,128)S(1)} %fusion.24, f32[128,128]{1,0:T(8,128)S(1)} %get-tuple-element.50, f32[128,128]{1,0:T(8,128)S(1)} %get-tuple-element.51), kind=kOutput, calls=%fused_computation.41 | convolution fusion | flops 1610645504 | bytes 6422528 | tf_op jit(solution)/shard_map/brc,cd->brd/dot_general | solution.py:52
  137.9 6.7 %fusion.22 = f32[4,128,1024]{2,1,0:T(8,128)S(1)} fusion(f32[4,512,128]{2,1,0:T(8,128)S(1)} %copy-done.6, f32[512,512]{1,0:T(8,128)S(1)} %get-tuple-element.48, f32[512,512]{1,0:T(8,128)S(1)} %copy-done.1), kind=kOutput, calls=%fused_computation.46 | convolution fusion | flops 3221749760 | bytes 5242880 | tf_op jit(solution)/shard_map/rk,bkc->brc/dot_general | solution.py:51
  144.6 5.0 %fusion.16 = f32[4,1024,256]{2,1,0:T(8,128)} fusion(f32[4,128,1024]{2,1,0:T(8,128)S(1)} %fusion.22, f32[128,128]{1,0:T(8,128)S(1)} %get-tuple-element.50, f32[128,128]{1,0:T(8,128)S(1)} %get-tuple-element.51), kind=kOutput, calls=%fused_computation.37 | convolution fusion | flops 1610645504 | bytes 6422528 | tf_op jit(solution)/shard_map/brc,cd->brd/dot_general | solution.py:52
  149.7 68.9 %all-to-all-done.1 = f32[16,2,512,128]{3,2,1,0:T(8,128)} async-done(((f32[16,2,512,128]{3,2,1,0:T(8,128)}), f32[16,2,512,128]{3,2,1,0:T(8,128)}, u32[]{:S(2)}, u32[]{:S(2)}) %all-to-all-start.1) | async-done | bytes 8388640 | tf_op jit(solution)/shard_map/all_to_all | solution.py:129
  218.6 7.6 %all-to-all-start.4 = ((s32[128,1,1,2]{3,2,1,0:T(1,128)}), s32[128,1,1,2]{3,2,1,0:T(1,128)S(1)}, u32[]{:S(2)}, u32[]{:S(2)}) async-start(s32[128,1,1,2]{3,2,1,0:T(1,128)} %bitcast.38), calls=%async_computation.4 | async-start | bytes 131072 | tf_op jit(solution)/shard_map/all_to_all | solution.py:34
  226.2 4.0 %gather_fusion.1 = f32[4,512,128]{2,1,0:T(8,128)S(1)} fusion(f32[32,512,128]{2,1,0:T(8,128)} %bitcast.16, s32[1024]{0:T(1024)S(1)} %pad_clamp_fusion.3), kind=kCustom, calls=%fused_computation.5 | custom fusion | bytes 2097168 | tf_op jit(solution)/shard_map/jit(_take)/gather | solution.py:104
  230.3 6.9 %fusion.23 = f32[4,128,1024]{2,1,0:T(8,128)S(1)} fusion(f32[4,512,128]{2,1,0:T(8,128)S(1)} %broadcast_select_fusion.1, f32[512,512]{1,0:T(8,128)S(1)} %get-tuple-element.48, f32[512,512]{1,0:T(8,128)S(1)} %copy-done.1), kind=kOutput, calls=%fused_computation.47 | convolution fusion | flops 3221749760 | bytes 5242880 | tf_op jit(solution)/shard_map/rk,bkc->brc/dot_general | solution.py:51
  256.8 4.1 %gather_fusion.7 = f32[4,512,128]{2,0,1:T(4,128)} fusion(f32[4,1024,128]{2,0,1:T(4,128)S(1)} %copy.71, s32[4]{0:T(128)S(1)} %get-tuple-element.37), kind=kCustom, calls=%fused_computation.clone | custom fusion | bytes 2097200 | tf_op jit(solution)/shard_map/vmap(jit(_roll_dynamic))/gather | solution.py:109
  272.9 8.5 %fusion.28 = f32[4]{0:T(128)S(1)} fusion(f32[512,512]{1,0:T(8,128)S(1)} %get-tuple-element.48, f32[512,512]{1,0:T(8,128)S(1)} %copy-done.2, f32[4,512,128]{2,1,0:T(8,128)} %get-tuple-element.31, f32[4,512,128]{2,1,0:T(8,128)} %get-tuple-element.30), kind=kOutput, calls=%fused_computation.50 | convolution fusion | flops 3222536192 | bytes 4194320 | tf_op jit(solution)/shard_map/rk,bkc->brc/dot_general | solution.py:75
  281.4 7.2 %fusion.25 = f32[4]{0:T(128)S(1)} fusion(f32[512,512]{1,0:T(8,128)S(1)} %get-tuple-element.48, f32[512,512]{1,0:T(8,128)S(1)} %copy-done.2, f32[4,512,128]{2,1,0:T(8,128)S(1)} %copy-done.11, f32[4,512,128]{2,1,0:T(8,128)S(1)} %copy-done.10), kind=kOutput, calls=%fused_computation.49 | convolution fusion | flops 3222536192 | bytes 4194320 | tf_op jit(solution)/shard_map/rk,bkc->brc/dot_general | solution.py:75
  295.8 10.2 %all-to-all-start.5 = ((f32[128,1,1,2,32,128]{5,4,3,2,1,0:T(8,128)}), f32[128,1,1,2,32,128]{5,4,3,2,1,0:T(8,128)}, u32[]{:S(2)}, u32[]{:S(2)}) async-start(f32[128,1,1,2,32,128]{5,4,3,2,1,0:T(8,128)} %select_select_fusion.1), calls=%async_computation.5 | async-start | bytes 8388608 | tf_op jit(solution)/shard_map/all_to_all | solution.py:34
  306.8 52.0 %all-to-all-done.5 = f32[128,1,1,2,32,128]{5,4,3,2,1,0:T(8,128)} async-done(((f32[128,1,1,2,32,128]{5,4,3,2,1,0:T(8,128)}), f32[128,1,1,2,32,128]{5,4,3,2,1,0:T(8,128)}, u32[]{:S(2)}, u32[]{:S(2)}) %all-to-all-start.5) | async-done | bytes 4194336 | tf_op jit(solution)/shard_map/all_to_all | solution.py:34
  358.8 7.9 %copy.88 = f32[32,8,32,128]{3,1,2,0:T(8,128)} copy(f32[32,8,32,128]{3,2,1,0:T(8,128)} %bitcast.72) | data formatting | bytes 8388608
  366.7 5.6 %copy.78 = f32[4096,256]{1,0:T(8,128)} copy(f32[4096,256]{0,1:T(8,128)} %bitcast.161) | data formatting | bytes 8388608 | tf_op jit(solution)/shard_map/dot_general | solution.py:175
  372.3 4.1 %fusion.50 = f32[16,32,128]{2,0,1:T(8,128)S(1)} fusion(f32[32,128,256]{2,1,0:T(8,128)} %bitcast.160, s32[256]{0:T(256)S(1)} %eq.173), kind=kOutput, calls=%fused_computation.111 | convolution fusion | flops 201330688 | bytes 4457472 | tf_op jit(solution)/shard_map/dot_general | solution.py:175
  (136 shorter events, 88.9 us)
Async XLA Ops:
  4.7 16.6 %all-to-all-start.2 = ((s32[8,1,2]{2,1,0:T(1,128)}), s32[8,1,2]{2,1,0:T(1,128)S(1)}, u32[]{:S(2)}, u32[]{:S(2)}) async-start(s32[8,1,2]{2,1,0:T(1,128)} %bitcast.28), calls=%async_computation.2 | async-start | bytes 8192 | tf_op jit(solution)/shard_map/all_to_all | solution.py:138
  21.3 14.0 %all-to-all-start = ((s32[16,1,2]{2,1,0:T(1,128)}), s32[16,1,2]{2,1,0:T(1,128)S(1)}, u32[]{:S(2)}, u32[]{:S(2)}) async-start(s32[16,1,2]{2,1,0:T(1,128)} %bitcast.13), calls=%async_computation | async-start | bytes 16384 | tf_op jit(solution)/shard_map/all_to_all | solution.py:130
  35.3 55.0 %all-to-all-start.3 = ((f32[8,2,512,128]{3,2,1,0:T(8,128)}), f32[8,2,512,128]{3,2,1,0:T(8,128)}, u32[]{:S(2)}, u32[]{:S(2)}) async-start(f32[8,2,512,128]{3,2,1,0:T(8,128)} %select_select_fusion.2), calls=%async_computation.3 | async-start | bytes 8388608 | tf_op jit(solution)/shard_map/all_to_all | solution.py:137
  54.4 41.6 %copy-start.13 = (s32[64]{0:T(128)S(1)}, s32[64]{0:T(128)}, u32[]{:S(2)}) copy-start(s32[64]{0:T(128)} %param.15) | copy-start | bytes 772
  90.3 128.3 %all-to-all-start.1 = ((f32[16,2,512,128]{3,2,1,0:T(8,128)}), f32[16,2,512,128]{3,2,1,0:T(8,128)}, u32[]{:S(2)}, u32[]{:S(2)}) async-start(f32[16,2,512,128]{3,2,1,0:T(8,128)} %select_select_fusion), calls=%async_computation.1 | async-start | bytes 16777216 | tf_op jit(solution)/shard_map/all_to_all | solution.py:129
  95.3 8.4 %copy-start.12 = (s32[2,2,4]{2,1,0:T(2,128)S(1)}, s32[2,2,4]{2,1,0:T(2,128)}, u32[]{:S(2)}) copy-start(s32[2,2,4]{2,1,0:T(2,128)} %param.13) | copy-start | bytes 196
  95.3 9.3 %copy-start.7 = (f32[4,512,128]{2,1,0:T(8,128)S(1)}, f32[4,512,128]{2,1,0:T(8,128)}, u32[]{:S(2)}) copy-start(f32[4,512,128]{2,1,0:T(8,128)} %param.9) | copy-start | bytes 3145732
  103.7 4.4 %copy-start = (f32[512,512]{1,0:T(8,128)}, f32[512,512]{1,0:T(8,128)S(1)}, u32[]{:S(2)}) copy-start(f32[512,512]{1,0:T(8,128)S(1)} %get-tuple-element.49) | copy-start | bytes 3145732
  118.6 1.0 copy-start.5
  135.2 2.7 copy-start.1
  135.2 2.7 copy-start.6
  218.6 77.3 %all-to-all-start.4 = ((s32[128,1,1,2]{3,2,1,0:T(1,128)}), s32[128,1,1,2]{3,2,1,0:T(1,128)S(1)}, u32[]{:S(2)}, u32[]{:S(2)}) async-start(s32[128,1,1,2]{3,2,1,0:T(1,128)} %bitcast.38), calls=%async_computation.4 | async-start | bytes 131072 | tf_op jit(solution)/shard_map/all_to_all | solution.py:34
  237.4 3.7 copy-start.3
  246.2 2.9 copy-start.4
  271.2 1.7 copy-start.2
  272.9 8.5 %copy-start.10 = (f32[4,512,128]{2,1,0:T(8,128)S(1)}, f32[4,512,128]{2,1,0:T(8,128)}, u32[]{:S(2)}) copy-start(f32[4,512,128]{2,1,0:T(8,128)} %get-tuple-element.32) | copy-start | bytes 3145732
  272.9 8.5 %copy-start.11 = (f32[4,512,128]{2,1,0:T(8,128)S(1)}, f32[4,512,128]{2,1,0:T(8,128)}, u32[]{:S(2)}) copy-start(f32[4,512,128]{2,1,0:T(8,128)} %get-tuple-element.33) | copy-start | bytes 3145732
  281.4 7.2 %copy-start.8 = (f32[4,512,128]{2,1,0:T(8,128)S(1)}, f32[4,512,128]{2,1,0:T(8,128)}, u32[]{:S(2)}) copy-start(f32[4,512,128]{2,1,0:T(8,128)} %param.9) | copy-start | bytes 3145732
  281.4 7.2 %copy-start.9 = (f32[4,512,128]{2,1,0:T(8,128)S(1)}, f32[4,512,128]{2,1,0:T(8,128)}, u32[]{:S(2)}) copy-start(f32[4,512,128]{2,1,0:T(8,128)} %copy.76) | copy-start | bytes 3145732
  295.8 62.9 %all-to-all-start.5 = ((f32[128,1,1,2,32,128]{5,4,3,2,1,0:T(8,128)}), f32[128,1,1,2,32,128]{5,4,3,2,1,0:T(8,128)}, u32[]{:S(2)}, u32[]{:S(2)}) async-start(f32[128,1,1,2,32,128]{5,4,3,2,1,0:T(8,128)} %select_select_fusion.1), calls=%async_computation.5 | async-start | bytes 8388608 | tf_op jit(solution)/shard_map/all_to_all | solution.py:34
where the time goes:
time: 383 us; the launch traced here: 377 us
  waiting for transfers between devices  158 us (41%)
  local copies, waits for them, and re-layouts  71.7 us (19%)
  matrix products  58.3 us (15%)
  other arithmetic  44.3 us (12%)
  starting transfers between devices  42.6 us (11%)
    all_to_all x1, waiting for transfers between devices, local(): lax.all_to_all(first_send, 'slab', split_axis=0, concat_axis=0, tiled=True)  68.9 us
    all_to_all x2, waiting for transfers between devices, one_exchange(): lax.all_to_all(blocks, axis, split_axis=0, concat_axis=0, tiled=True)  52 us
    all_to_all x1, waiting for transfers between devices, local(): lax.all_to_all(second_send, 'tile', split_axis=0, concat_axis=0, tiled=True)  35.9 us
    gather x6, local copies, waits for them, and re-layouts, shift_planes(): jnp.roll(plane, (first_shift, second_shift), axis=(0, 1))  20.2 us
    all_to_all x2, starting transfers between devices, one_exchange(): lax.all_to_all(blocks, axis, split_axis=0, concat_axis=0, tiled=True)  17.8 us
    dot_general x3, matrix products, forward(): halves = jnp.einsum('rk,bkc->brc', stacked, planes, precision=HIGHEST)  17.1 us
    select_n x3, other arithmetic, pack(): jnp.where(filled.reshape((-1,) + (1,) * (values.ndim - 1)), gathered, 0.0)  17.1 us
    dot_general x2, matrix products, inverse(): jnp.einsum('rk,bkc->brc', stacked, jnp.concatenate([first_real, first_ima...  15.7 us
  transfers between devices with their start and end apart: 6, of which 4 were waited for; matrix products, arithmetic and copies ran while one was open for 40% of the time, Pallas kernels for 0%

commit v1 on v0

v1 whole, which is shorter than its diff:
```python
import functools
import math

import jax
import jax.numpy as jnp
import ml_dtypes
import numpy as np
from jax import lax
from jax.experimental import pallas as pl
from jax.experimental.pallas import tpu as pltpu
from jax.sharding import PartitionSpec as P

MESH = pl.DeviceIdType.MESH
F32 = jnp.float32
BF16 = jnp.bfloat16
H = 512
W = 128
STRIPS = 4
PIECES = 16
BAND = H // PIECES
OWNED = 16
HALF = H // 2
SPEC = HALF + 8
PAD = BAND + 8


def halves_of(table):
    high = table.astype(ml_dtypes.bfloat16)
    low = (table - high.astype(np.float64)).astype(ml_dtypes.bfloat16)
    return jnp.asarray(high), jnp.asarray(low)


def tables():
    n = np.arange(HALF)
    even = np.arange(0, HALF, 2)
    odd = np.arange(1, HALF, 2)
    row_scale = 1.0 / math.sqrt(H)

    def cos_rows(k):
        return np.cos(2 * np.pi * ((k[:, None] * n[None, :]) % H) / H) * row_scale

    def sin_rows(k):
        return np.sin(2 * np.pi * ((k[:, None] * n[None, :]) % H) / H) * row_scale

    last = np.zeros((8, HALF))
    last[0] = np.where(n % 2 == 0, 1.0, -1.0) * row_scale
    forward_even = np.concatenate([cos_rows(even), last, -sin_rows(even)], 0)
    forward_odd = np.concatenate([cos_rows(odd), -sin_rows(odd)], 0)
    re_part = 2 * cos_rows(even)
    re_part[0] *= 0.5
    im_part = -2 * sin_rows(even)
    im_part[0] = last[0]
    back_even = np.concatenate([re_part, im_part], 0).T
    back_odd = np.concatenate([2 * cos_rows(odd), -2 * sin_rows(odd)], 0).T
    m = np.arange(W)
    angle = 2 * np.pi * ((m[:, None] * m[None, :]) % W) / W
    c, s = np.cos(angle) / math.sqrt(W), np.sin(angle) / math.sqrt(W)
    column_forward = np.block([[c, -s], [s, c]])
    column_back = np.block([[c, s], [-s, c]])
    parts = []
    for table in (forward_even, forward_odd, column_forward, column_back, back_even, back_odd):
        parts.extend(halves_of(table))
    return parts


def split(x):
    high = x.astype(BF16)
    return high, (x - high.astype(F32)).astype(BF16)


def dot(a, b):
    return jnp.dot(a, b, preferred_element_type=F32)


def left(high, low, x):
    xh, xl = split(x)
    return dot(high[...], xh) + (dot(low[...], xh) + dot(high[...], xl))


def right(x, high, low):
    xh, xl = split(x)
    return dot(xh, high[...]) + (dot(xl, high[...]) + dot(xh, low[...]))


def exchange_kernel(
    slabs, tiles, moving, codes, partner, got0, got1, pick0, pick1, code0, code1, inv_v, inv_s,
    send_a, recv_a, send_b, recv_b, send_c, recv_c, own_sem,
):
    p = lax.axis_index("slab")
    q = lax.axis_index("tile")
    groups = (("slab", slabs, p, got0, pick0, code0), ("tile", tiles, q, got1, pick1, code1))

    barrier = pltpu.get_barrier_semaphore()
    for axis, size, me, _, _, _ in groups:
        for step in range(1, size):
            pl.semaphore_signal(
                barrier, inc=1, device_id={axis: lax.rem(me + step, size)}, device_id_type=MESH
            )
    pl.semaphore_wait(barrier, slabs + tiles - 2)

    def code_copy(r, step):
        axis, size, me, _, _, code = groups[r]
        peer = lax.rem(me + step, size)
        base = r * slabs + step
        return pltpu.make_async_remote_copy(
            src_ref=codes.at[r], dst_ref=code.at[me], send_sem=send_c.at[base],
            recv_sem=recv_c.at[base], device_id={axis: peer}, device_id_type=MESH,
        )

    def spread_copy(r, step):
        axis, size, me, got, _, _ = groups[r]
        peer = lax.rem(me + step, size)
        rows = H // size
        base = r * slabs + step
        return pltpu.make_async_remote_copy(
            src_ref=moving.at[r, :, pl.ds(pl.multiple_of(peer * rows, rows), rows), :],
            dst_ref=got.at[pl.ds(me * STRIPS, STRIPS)],
            send_sem=send_a.at[base], recv_sem=recv_a.at[base],
            device_id={axis: peer}, device_id_type=MESH,
        )

    def gather_copy(r, step):
        axis, size, me, _, pick, _ = groups[r]
        peer = lax.rem(me + step, size)
        rows = H // size
        base = r * slabs + step
        return pltpu.make_async_remote_copy(
            src_ref=pick.at[pl.ds(peer * STRIPS, STRIPS)],
            dst_ref=partner.at[r, :, pl.ds(pl.multiple_of(me * rows, rows), rows), :],
            send_sem=send_b.at[base], recv_sem=recv_b.at[base],
            device_id={axis: peer}, device_id_type=MESH,
        )

    own = []
    for r, (axis, size, me, got, _, code) in enumerate(groups):
        rows = H // size
        for step in range(1, size):
            code_copy(r, step).start()
        own.append(pltpu.make_async_copy(
            moving.at[r, :, pl.ds(pl.multiple_of(me * rows, rows), rows), :],
            got.at[pl.ds(me * STRIPS, STRIPS)], own_sem.at[r]))
        own.append(pltpu.make_async_copy(codes.at[r], code.at[me], own_sem.at[2 + r]))
    for copy in own:
        copy.start()
    for step in range(1, slabs):
        spread_copy(0, step).start()
        if step < tiles:
            spread_copy(1, step).start()

    for r, (axis, size, me, got, pick, code) in enumerate(groups):
        own[2 * r + 1].wait()
        for step in range(1, size):
            code_copy(r, step).wait()
        lane = lax.broadcasted_iota(jnp.int32, (8, W), 1)
        row = lax.broadcasted_iota(jnp.int32, (8, W), 0)
        total = jnp.zeros((8, W), jnp.int32)
        for i in range(size):
            total += jnp.where(code[i] == lane, i * STRIPS + row, 0)
        source = jnp.minimum(jnp.sum(total, 0, keepdims=True), size * STRIPS - 1)
        inv_v[r] = jnp.broadcast_to(source, (8, W))
    table = pltpu.make_async_copy(inv_v, inv_s, own_sem.at[4])
    table.start()
    table.wait()

    final = []
    for r in (1, 0):
        axis, size, me, got, pick, code = groups[r]
        rows = H // size
        own[2 * r].wait()
        for step in range(1, size):
            spread_copy(r, step).wait()
        for step in list(range(1, size)) + [0]:
            peer = lax.rem(me + step, size)
            for s in range(STRIPS):
                pick[peer * STRIPS + s] = got[inv_s[r, 0, peer * STRIPS + s]]
            if step:
                gather_copy(r, step).start()
        final.append(pltpu.make_async_copy(
            pick.at[pl.ds(me * STRIPS, STRIPS)],
            partner.at[r, :, pl.ds(pl.multiple_of(me * rows, rows), rows), :], own_sem.at[5 + r]))
        final[-1].start()
    for copy in final:
        copy.wait()
    for r in (1, 0):
        for step in range(1, groups[r][1]):
            gather_copy(r, step).wait()


def exchange(moving, codes, slabs, tiles):
    count = slabs + tiles
    return pl.pallas_call(
        functools.partial(exchange_kernel, slabs, tiles),
        out_shape=jax.ShapeDtypeStruct((2, STRIPS, H, W), F32),
        in_specs=[pl.BlockSpec(memory_space=pl.ANY), pl.BlockSpec(memory_space=pltpu.VMEM)],
        out_specs=pl.BlockSpec(memory_space=pl.ANY),
        scratch_shapes=[
            pltpu.VMEM((slabs * STRIPS, H // slabs, W), F32),
            pltpu.VMEM((tiles * STRIPS, H // tiles, W), F32),
            pltpu.VMEM((slabs * STRIPS, H // slabs, W), F32),
            pltpu.VMEM((tiles * STRIPS, H // tiles, W), F32),
            pltpu.VMEM((slabs, 8, W), jnp.int32),
            pltpu.VMEM((tiles, 8, W), jnp.int32),
            pltpu.VMEM((2, 8, W), jnp.int32),
            pltpu.SMEM((2, 8, W), jnp.int32),
        ]
        + [pltpu.SemaphoreType.DMA((count,))] * 6
        + [pltpu.SemaphoreType.DMA((8,))],
        compiler_params=pltpu.CompilerParams(collective_id=0, has_side_effects=True),
        name="exchange_rounds",
    )(moving, codes)


def merge_kernel(
    shifts, live, fixed, partner, fe_h, fe_l, fo_h, fo_l, cf_h, cf_l, cb_h, cb_l, be_h, be_l,
    bo_h, bo_l, peaks, spread, merged,
):
    s = pl.program_id(0)
    x = jnp.concatenate([fixed[0], partner[0, 0], partner[1, 0]], 1)
    u = left(fe_h, fe_l, x[:HALF] + x[HALF:])
    v = left(fo_h, fo_l, x[:HALF] - x[HALF:])
    quarter = HALF // 2
    joined = []
    for i in range(3):
        lanes = slice(W * i, W * (i + 1))
        re_part = jnp.concatenate(
            [u[:quarter, lanes], v[:quarter, lanes], u[quarter : quarter + 8, lanes]], 0)
        im_part = jnp.concatenate(
            [u[quarter + 8 :, lanes], v[quarter:, lanes], jnp.zeros((8, W), F32)], 0)
        joined.append(jnp.concatenate([re_part, im_part], 1))
    spectra = right(jnp.concatenate(joined, 0), cf_h, cf_l)
    fr, fi = spectra[:SPEC, :W], spectra[:SPEC, W:]
    crossed = []
    for i in (1, 2):
        gr, gi = spectra[SPEC * i : SPEC * (i + 1), :W], spectra[SPEC * i : SPEC * (i + 1), W:]
        cr = fr * gr + fi * gi
        ci = fi * gr - fr * gi
        scale = lax.rsqrt(cr * cr + ci * ci + 0.0625)
        crossed.append(jnp.concatenate([cr * scale, ci * scale], 1))
    back = right(jnp.concatenate(crossed, 0), cb_h, cb_l)
    evens, odds = [], []
    first = lax.broadcasted_iota(jnp.int32, (8, W), 0) == 0
    for i in range(2):
        pr, pi = back[SPEC * i : SPEC * (i + 1), :W], back[SPEC * i : SPEC * (i + 1), W:]
        evens.append(jnp.concatenate(
            [pr[:quarter], jnp.where(first, pr[HALF:], pi[:8]), pi[8:quarter]], 0))
        odds.append(jnp.concatenate([pr[quarter:HALF], pi[quarter:HALF]], 0))
    even = left(be_h, be_l, jnp.concatenate(evens, 1))
    odd = left(bo_h, bo_l, jnp.concatenate(odds, 1))
    surface = even + jnp.abs(odd)
    is_live = s < live[0]
    total = jnp.ones((1, 1), F32)
    acc = fixed[0]
    for r in range(2):
        peak = jnp.max(surface[:, W * r : W * (r + 1)], axis=(0, 1), keepdims=True)
        weight = 1.0 / (1.0 + jnp.exp(4.0 - peak))
        down = lax.rem(shifts[r, 0, s] + H, H)
        side = lax.rem(shifts[r, 1, s] + W, W)
        moved = pltpu.roll(pltpu.roll(partner[r, 0], side, 1), down, 0)
        acc = acc + weight * moved
        total = total + weight
        peaks[0, r : r + 1, :] = jnp.broadcast_to(jnp.where(is_live, peak, 0.0), (1, W))
    peaks[0, 2:8, :] = jnp.zeros((6, W), F32)
    acc = jnp.where(is_live, acc * (1.0 / total), 0.0)
    for k in range(PIECES):
        merged[pl.ds(k * PAD, BAND), :] = acc[k * BAND : (k + 1) * BAND]
    for r in range(BAND):
        spread[r] = merged[pl.ds(r, PIECES, stride=PAD), :]


def merge(shifts, live, fixed, partner):
    parts = tables()
    whole = lambda t: pl.BlockSpec(t.shape, lambda s: (0, 0))
    return pl.pallas_call(
        merge_kernel,
        grid=(STRIPS,),
        out_shape=(
            jax.ShapeDtypeStruct((STRIPS, 8, W), F32),
            jax.ShapeDtypeStruct((BAND, STRIPS * PIECES, W), F32),
        ),
        in_specs=[
            pl.BlockSpec(memory_space=pltpu.SMEM),
            pl.BlockSpec(memory_space=pltpu.SMEM),
            pl.BlockSpec((1, H, W), lambda s: (s, 0, 0)),
            pl.BlockSpec((2, 1, H, W), lambda s: (0, s, 0, 0)),
        ]
        + [whole(t) for t in parts],
        out_specs=(
            pl.BlockSpec((1, 8, W), lambda s: (s, 0, 0)),
            pl.BlockSpec((BAND, PIECES, W), lambda s: (0, s, 0)),
        ),
        scratch_shapes=[pltpu.VMEM((PIECES * PAD, W), F32)],
        name="correlate_merge",
    )(shifts, live, fixed, partner, *parts)


def rows_kernel(slabs, tiles, inner, spread, labels, got, got_labels, send_a, recv_a, send_b, recv_b, own_sem):
    p = lax.axis_index("slab")
    q = lax.axis_index("tile")
    size = inner * tiles
    base = (p // inner) * inner
    me = lax.rem(p, inner) * tiles + q

    def place(step):
        peer = lax.rem(me + step, size)
        return peer, (base + peer // tiles, lax.rem(peer, tiles))

    barrier = pltpu.get_barrier_semaphore()
    for step in range(1, size):
        pl.semaphore_signal(barrier, inc=1, device_id=place(step)[1], device_id_type=MESH)
    pl.semaphore_wait(barrier, size - 1)

    def data(step):
        peer, device = place(step)
        return pltpu.make_async_remote_copy(
            src_ref=spread.at[peer], dst_ref=got.at[me], send_sem=send_a.at[step],
            recv_sem=recv_a.at[step], device_id=device, device_id_type=MESH)

    def label(step):
        _, device = place(step)
        return pltpu.make_async_remote_copy(
            src_ref=labels, dst_ref=got_labels.at[me], send_sem=send_b.at[step],
            recv_sem=recv_b.at[step], device_id=device, device_id_type=MESH)

    own_data = pltpu.make_async_copy(spread.at[me], got.at[me], own_sem.at[0])
    own_label = pltpu.make_async_copy(labels, got_labels.at[me], own_sem.at[1])
    for step in range(1, size):
        label(step).start()
        data(step).start()
    own_data.start()
    own_label.start()
    own_data.wait()
    own_label.wait()
    for step in range(1, size):
        label(step).wait()
        data(step).wait()


def rows_exchange(spread, labels, slabs, tiles):
    inner = BAND // tiles
    return pl.pallas_call(
        functools.partial(rows_kernel, slabs, tiles, inner),
        out_shape=(
            jax.ShapeDtypeStruct((BAND, STRIPS * PIECES, W), F32),
            jax.ShapeDtypeStruct((BAND, 1, W), jnp.int32),
        ),
        in_specs=[pl.BlockSpec(memory_space=pltpu.VMEM), pl.BlockSpec(memory_space=pltpu.VMEM)],
        out_specs=(pl.BlockSpec(memory_space=pltpu.VMEM), pl.BlockSpec(memory_space=pltpu.VMEM)),
        scratch_shapes=[pltpu.SemaphoreType.DMA((BAND,))] * 4 + [pltpu.SemaphoreType.DMA((2,))],
        compiler_params=pltpu.CompilerParams(collective_id=1, has_side_effects=True),
        name="spread_rows",
    )(spread, labels)


BANKS = 8


def sum_kernel(got, labels, sums, *banks):
    blocks = sums.shape[0]
    zero = jnp.zeros((64, W), F32)

    def clear(i, carry):
        for bank in banks:
            bank[pl.ds(pl.multiple_of(i * 64, 64), 64), :] = zero
        return carry

    lax.fori_loop(0, blocks // 64, clear, 0)
    per = got.shape[1] // BANKS

    def add(i, carry):
        d = i // per
        k = lax.rem(i, per) * BANKS
        for b, bank in enumerate(banks):
            block = labels[d, 0, k + b]
            bank[pl.ds(block, 1), :] += got[d, pl.ds(k + b, 1), :]
        return carry

    lax.fori_loop(0, got.shape[0] * per, add, 0)

    def fold(i, carry):
        at = pl.ds(pl.multiple_of(i * 64, 64), 64)
        parts = [bank[at, :] for bank in banks]
        while len(parts) > 1:
            parts = [parts[j] + parts[j + 1] for j in range(0, len(parts), 2)]
        sums[at, :] = parts[0]
        return carry

    lax.fori_loop(0, blocks // 64, fold, 0)


def sum_blocks(got, labels, blocks):
    return pl.pallas_call(
        sum_kernel,
        out_shape=jax.ShapeDtypeStruct((blocks, W), F32),
        in_specs=[pl.BlockSpec(memory_space=pltpu.VMEM), pl.BlockSpec(memory_space=pltpu.SMEM)],
        out_specs=pl.BlockSpec(memory_space=pltpu.VMEM),
        scratch_shapes=[pltpu.VMEM((blocks, W), F32)] * BANKS,
        name="sum_blocks",
    )(got, labels)


def owners_kernel(slabs, tiles, sums, out, got, send_sem, recv_sem, own_sem):
    p = lax.axis_index("slab")
    q = lax.axis_index("tile")
    size = slabs * tiles
    me = p * tiles + q

    def place(step):
        peer = lax.rem(me + step, size)
        return peer, (peer // tiles, lax.rem(peer, tiles))

    barrier = pltpu.get_barrier_semaphore()

    def greet(step, carry):
        pl.semaphore_signal(barrier, inc=1, device_id=place(step)[1], device_id_type=MESH)
        return carry

    lax.fori_loop(1, size, greet, 0)
    pl.semaphore_wait(barrier, size - 1)

    def copy(step):
        peer, device = place(step)
        return pltpu.make_async_remote_copy(
            src_ref=sums.at[peer], dst_ref=got.at[me], send_sem=send_sem.at[step],
            recv_sem=recv_sem.at[step], device_id=device, device_id_type=MESH)

    def start(step, carry):
        copy(step).start()
        return carry

    def wait(step, carry):
        copy(step).wait()
        return carry

    lax.fori_loop(1, size, start, 0)
    got[me] = sums[me]
    lax.fori_loop(1, size, wait, 0)
    for r in range(BAND):
        total = got[r]
        for z in range(1, size // BAND):
            total = total + got[z * BAND + r]
        out[:, r, :] = total


def to_owners(sums, slabs, tiles):
    size = slabs * tiles
    return pl.pallas_call(
        functools.partial(owners_kernel, slabs, tiles),
        out_shape=jax.ShapeDtypeStruct((OWNED, BAND, W), F32),
        in_specs=[pl.BlockSpec(memory_space=pltpu.VMEM)],
        out_specs=pl.BlockSpec(memory_space=pltpu.VMEM),
        scratch_shapes=[
            pltpu.VMEM((size, OWNED, W), F32),
            pltpu.SemaphoreType.DMA((size,)),
            pltpu.SemaphoreType.DMA((size,)),
            pltpu.SemaphoreType.DMA((1,)),
        ],
        compiler_params=pltpu.CompilerParams(collective_id=2, has_side_effects=True),
        name="rows_to_owners",
    )(sums)


def local(slabs, tiles, fixed, moving, pair_dest, pair_slot, plane_shift, live_count, piece_block):
    codes = pair_dest * STRIPS + pair_slot
    codes = jnp.concatenate([codes, jnp.full((2, 8 - STRIPS), -1, jnp.int32)], 1)
    codes = jnp.broadcast_to(codes[:, :, None], (2, 8, W))
    partner = exchange(moving, codes, slabs, tiles)
    peaks, spread = merge(plane_shift, live_count, fixed, partner)
    labels = jnp.pad(piece_block, (0, W - piece_block.shape[0])).reshape(1, W)
    got, got_labels = rows_exchange(spread, labels, slabs, tiles)
    size = slabs * tiles
    sums = sum_blocks(got, got_labels, size * OWNED)
    blocks = to_owners(sums.reshape(size, OWNED, W), slabs, tiles)
    return peaks[:, :2, 0].T, blocks


def solution(mesh):
    both = ("slab", "tile")
    placed = (
        P(both, None, None),
        P(None, both, None, None),
        P(None, both),
        P(None, both),
        P(None, None, both),
        P(both),
        P(both),
    )
    return jax.shard_map(
        functools.partial(local, mesh.shape["slab"], mesh.shape["tile"]),
        mesh=mesh,
        in_specs=placed,
        out_specs=(P(None, both), P(both, None, None)),
        check_vma=False,
    )
```

time: 383 us -> 123 us (0.32); the launches traced: 377 us -> 123 us
  waiting for transfers between devices: 158 us -> 0 us
  Pallas kernels: 0 us -> 117 us
  local copies, waits for them, and re-layouts: 71.7 us -> 4.25 us
  matrix products: 58.3 us -> 0 us
  other arithmetic: 44.3 us -> 0.7 us
  starting transfers between devices: 42.6 us -> 0 us
    all_to_all x6 -> x0, waiting for transfers between devices: 158 us -> none  [the longest x1 68.9 us: local(): lax.all_to_all(first_send, 'slab', split_axis=0, concat_axis=0, tiled=True)]
    pallas_call x0 -> x5, Pallas kernels: none -> 117 us  [the longest x1 39.7 us: exchange(): pl.pallas_call(functools.partial(exchange_kernel, slabs, tiles), out_shap...]
    dot_general x11 -> x0, matrix products: 58.3 us -> none  [the longest x3 17.1 us: forward(): halves = jnp.einsum('rk,bkc->brc', stacked, planes, precision=HIGHEST)]
    all_to_all x6 -> x0, starting transfers between devices: 42.6 us -> none  [the longest x2 17.8 us: one_exchange(): lax.all_to_all(blocks, axis, split_axis=0, concat_axis=0, tiled=True)]
    gather x17 -> x0, local copies, waits for them, and re-layouts: 41.3 us -> none  [the longest x6 20.2 us: shift_planes(): jnp.roll(plane, (first_shift, second_shift), axis=(0, 1))]
    select_n x17 -> x0, other arithmetic: 19.4 us -> none  [the longest x3 17.1 us: pack(): jnp.where(filled.reshape((-1,) + (1,) * (values.ndim - 1)), gathered, 0.0)]
    unnamed x30 -> x3, local copies, waits for them, and re-layouts: 11.2 us -> 1.68 us
    concatenate x4 -> x1, local copies, waits for them, and re-layouts: 8.45 us -> 0.01 us  [local(): jnp.concatenate([codes, jnp.full((2, 8 - STRIPS), -1, jnp.int32)], 1)]
  transfers between devices with their start and end apart: 6 -> 0, of which waited for: 4 -> 0; matrix products, arithmetic and copies ran while one was open for 40% -> 0% of each run, Pallas kernels for 0% -> 0%
where the time goes in v1:
time: 123 us
  Pallas kernels  117 us (95%)
  local copies, waits for them, and re-layouts  4.25 us (3%)
  between operations  1.32 us (1%)
    pallas_call x1, Pallas kernels, exchange(): pl.pallas_call(functools.partial(exchange_kernel, slabs, tiles), out_shap...  39.7 us
    pallas_call x1, Pallas kernels, to_owners(): pl.pallas_call(functools.partial(owners_kernel, slabs, tiles), out_shape=...  31.8 us
    pallas_call x1, Pallas kernels, rows_exchange(): pl.pallas_call(functools.partial(rows_kernel, slabs, tiles, inner), out_s...  21.6 us
    pallas_call x1, Pallas kernels, merge(): pl.pallas_call(merge_kernel, grid=(STRIPS,), out_shape=(jax.ShapeDtypeStr...  12.9 us
    pallas_call x1, Pallas kernels, sum_blocks(): pl.pallas_call(sum_kernel, out_shape=jax.ShapeDtypeStruct((blocks, W), F3...  10.5 us

profile of v1, /device:TPU:1, one launch (start us, length us, event | category | flops | bytes accessed | tf_op | source)
XLA Modules:
  0.0 122.8 jit_solution(15269920198264469544)
XLA Ops:
  0.6 0.7 multiply_add_fusion
  1.3 0.7 broadcast_in_dim.2.codes
  2.0 39.7 %exchange_rounds.1.partner = f32[2,4,512,128]{3,2,1,0:T(8,128)} custom-call(f32[2,4,512,128]{3,2,1,0:T(8,128)} %moving.1, s32[2,8,128]{2,1,0:T(8,128)} %broadcast_in_dim.2.codes), custom_call_target="tpu_custom_call" | custom-call | tf_op jit(solution)/shard_map/exchange_rounds/pallas_call | solution.py:191
  42.4 0.0 copy-start
  42.4 12.9 %correlate_merge.1 = (f32[4,8,128]{2,1,0:T(8,128)}, f32[32,64,128]{2,1,0:T(8,128)}) custom-call(s32[2,2,4]{2,1,0:T(2,128)} %shifts.1, s32[1]{0:T(128)S(6)} %copy.23.live, f32[4,512,128]{2,1,0:T(8,128)} %fixed.1, f32[2,4,512,128]{3,2,1,0:T(8,128)} %exchange_rounds.1.partner, bf16[264,256]{1,0:T(8,128)(2,1)} %constant.30.clone.fe_h, ...), custom_call_target="tpu_custom_call" | custom-call | tf_op jit(solution)/shard_map/correlate_merge/pallas_call | solution.py:273
  55.2 0.0 copy-done
  55.2 0.5 pad_bitcast_fusion.labels
  55.7 21.6 %spread_rows.1 = (f32[32,64,128]{2,1,0:T(8,128)}, s32[32,1,128]{2,1,0:T(1,128)}) custom-call(f32[32,64,128]{2,1,0:T(8,128)} %get-tuple-element.7.spread, s32[1,128]{1,0:T(1,128)} %pad_bitcast_fusion.labels), custom_call_target="tpu_custom_call" | custom-call | tf_op jit(solution)/shard_map/spread_rows/pallas_call | solution.py:340
  77.4 10.5 %sum_blocks.1 = f32[2048,128]{1,0:T(8,128)} custom-call(f32[32,64,128]{2,1,0:T(8,128)} %get-tuple-element.8.got, s32[32,1,128]{2,1,0:T(1,128)} %get-tuple-element.9.labels), custom_call_target="tpu_custom_call" | custom-call | tf_op jit(solution)/shard_map/sum_blocks/pallas_call | solution.py:391
  87.9 31.8 %rows_to_owners.1 = f32[16,32,128]{2,1,0:T(8,128)} custom-call(f32[128,16,128]{2,1,0:T(8,128)} %bitcast.6), custom_call_target="tpu_custom_call" | custom-call | tf_op jit(solution)/shard_map/rows_to_owners/pallas_call | solution.py:446
  119.7 0.7 slice.3
  120.5 0.7 copy.21
  121.1 1.7 %copy.24 = f32[16,32,128]{2,1,0:T(8,128)} copy(f32[16,32,128]{2,1,0:T(8,128)} %rows_to_owners.1) | data formatting | bytes 524288
  (1 shorter events, 0.0 us)
Async XLA Ops:
  42.4 12.9 %copy-start = (s32[64]{0:T(128)S(1)}, s32[64]{0:T(128)}, u32[]{:S(2)}) copy-start(s32[64]{0:T(128)} %param.25) | copy-start | bytes 772

commit v2 on v0

v2 whole, which is shorter than its diff:
```python
import functools
import math

import jax
import jax.numpy as jnp
import ml_dtypes
import numpy as np
from jax import lax
from jax.experimental import pallas as pl
from jax.experimental.pallas import tpu as pltpu
from jax.sharding import PartitionSpec as P

MESH = pl.DeviceIdType.MESH
F32 = jnp.float32
BF16 = jnp.bfloat16
H = 512
W = 128
STRIPS = 4
PIECES = 16
BAND = H // PIECES
OWNED = 16
HALF = H // 2
QUARTER = HALF // 2
SPEC = HALF + 8
PAD = BAND + 8
RING = 4
FIRST = HALF + 16


def tables():
    n = np.arange(HALF)
    even = np.arange(0, HALF, 2)
    odd = np.arange(1, HALF, 2)
    row_scale = 1.0 / math.sqrt(H)

    def cos_rows(k):
        return np.cos(2 * np.pi * ((k[:, None] * n[None, :]) % H) / H) * row_scale

    def sin_rows(k):
        return np.sin(2 * np.pi * ((k[:, None] * n[None, :]) % H) / H) * row_scale

    last = np.zeros((16, HALF))
    last[0] = np.where(n % 2 == 0, 1.0, -1.0) * row_scale
    forward_even = np.concatenate([cos_rows(even), last, -sin_rows(even)], 0)
    forward_odd = np.concatenate([cos_rows(odd), -sin_rows(odd)], 0)
    re_part = 2 * cos_rows(even)
    re_part[0] *= 0.5
    im_part = -2 * sin_rows(even)
    im_part[0] = last[0]
    back_even = np.concatenate([re_part, im_part], 0).T
    back_odd = np.concatenate([2 * cos_rows(odd), -2 * sin_rows(odd)], 0).T
    m = np.arange(W)
    angle = 2 * np.pi * ((m[:, None] * m[None, :]) % W) / W
    c, s = np.cos(angle) / math.sqrt(W), np.sin(angle) / math.sqrt(W)
    column_forward = np.block([[c, -s], [s, c]])
    column_back = np.block([[c, s], [-s, c]])
    table = np.concatenate(
        [forward_even, forward_odd, column_forward, column_back, back_even, back_odd], 0
    )
    high = table.astype(ml_dtypes.bfloat16)
    low = (table - high.astype(np.float64)).astype(ml_dtypes.bfloat16)
    return jnp.asarray(np.stack([high, low]))


TABLE_ROWS = FIRST + 5 * HALF


def dot(a, b):
    return jnp.dot(a, b, preferred_element_type=F32)


def split(x):
    high = x.astype(BF16)
    return high, (x - high.astype(F32)).astype(BF16)


def part(table, index):
    start, rows = (0, FIRST) if index == 0 else (FIRST + HALF * (index - 1), HALF)
    return table[0, start : start + rows, :], table[1, start : start + rows, :]


def left(table, index, x):
    high, low = part(table, index)
    xh, xl = split(x)
    return dot(high, xh) + (dot(low, xh) + dot(high, xl))


def right(x, table, index):
    high, low = part(table, index)
    xh, xl = split(x)
    return dot(xh, high) + (dot(xl, high) + dot(xh, low))


def forward_pair(table, a, b):
    x = jnp.concatenate([a, b], 1)
    u = left(table, 0, x[:HALF] + x[HALF:])
    v = left(table, 1, x[:HALF] - x[HALF:])
    joined = []
    for i in range(2):
        lanes = slice(W * i, W * (i + 1))
        re_part = jnp.concatenate(
            [u[:QUARTER, lanes], v[:QUARTER, lanes], u[QUARTER : QUARTER + 8, lanes]], 0)
        im_part = jnp.concatenate(
            [u[QUARTER + 16 :, lanes], v[QUARTER:, lanes], jnp.zeros((8, W), F32)], 0)
        joined.append(jnp.concatenate([re_part, im_part], 1))
    return right(jnp.concatenate(joined, 0), table, 2)


def surfaces(table, fixed_spectrum, spectra):
    fr, fi = fixed_spectrum[:, :W], fixed_spectrum[:, W:]
    crossed = []
    for i in range(2):
        gr, gi = spectra[SPEC * i : SPEC * (i + 1), :W], spectra[SPEC * i : SPEC * (i + 1), W:]
        cr = fr * gr + fi * gi
        ci = fi * gr - fr * gi
        scale = lax.rsqrt(cr * cr + ci * ci + 0.0625)
        crossed.append(jnp.concatenate([cr * scale, ci * scale], 1))
    back = right(jnp.concatenate(crossed, 0), table, 3)
    evens, odds = [], []
    first = lax.broadcasted_iota(jnp.int32, (8, W), 0) == 0
    for i in range(2):
        pr, pi = back[SPEC * i : SPEC * (i + 1), :W], back[SPEC * i : SPEC * (i + 1), W:]
        evens.append(jnp.concatenate(
            [pr[:QUARTER], jnp.where(first, pr[HALF:], pi[:8]), pi[8:QUARTER]], 0))
        odds.append(jnp.concatenate([pr[QUARTER:HALF], pi[QUARTER:HALF]], 0))
    even = left(table, 4, jnp.concatenate(evens, 1))
    odd = left(table, 5, jnp.concatenate(odds, 1))
    return even + jnp.abs(odd)


def far_first(*sizes):
    grid = [[]]
    for size in sizes:
        grid = [g + [v] for g in grid for v in range(size)]
    grid = [tuple(g) for g in grid if any(g)]

    def hops(g):
        return sum(min(v, RING - v) for v in g[:-1]) + (
            min(g[-1], RING - g[-1]) if sizes[-1] == RING else 0.25 * g[-1])

    return sorted(grid, key=lambda g: (-hops(g), g))


def whole_kernel(
    slabs, tiles, dest, slot, shifts, live, labels, moving, fixed_in, table_in, peaks, out,
    fixed, table, got0, got1, pick0, pick1, partner, code0, code1, inv_v, inv_s, fixed_spec,
    merged, spread, rows_got, label_got, onehot, sums, owned,
    send_sem, spread_sem, code_sem, label_sem, slot_sem, rows_sem, own_sem, owner_sem, ready,
):
    p = lax.axis_index("slab")
    q = lax.axis_index("tile")
    z, x = p // RING, lax.rem(p, RING)
    y, c = q // 2, lax.rem(q, 2)
    me = p * tiles + q
    member = lax.rem(me, BAND)
    devices = slabs * tiles
    axes = ("slab", "tile")
    sizes = (slabs, tiles)
    mine = (p, q)
    got = (got0, got1)
    pick = (pick0, pick1)
    code = (code0, code1)
    rows = (H // slabs, H // tiles)

    def slab_peer(g):
        return lax.rem(z + g[0], RING) * RING + lax.rem(x + g[1], RING)

    def tile_peer(g):
        return lax.rem(y + g[0], RING) * 2 + lax.rem(c + g[1], 2)

    peers = (
        [slab_peer(g) for g in far_first(RING, RING)],
        [tile_peer(g) for g in far_first(RING, 2)],
    )

    def local_wait(ref, sem):
        pltpu.make_async_copy(ref, ref, sem).wait()

    row8 = lax.broadcasted_iota(jnp.int32, (8, W), 0)
    lane8 = lax.broadcasted_iota(jnp.int32, (8, W), 1)

    barrier = pltpu.get_barrier_semaphore()
    for r in range(2):
        for peer in peers[r]:
            pl.semaphore_signal(barrier, inc=1, device_id={axes[r]: peer}, device_id_type=MESH)
    for r in range(2):
        tile = jnp.full((8, W), -1, jnp.int32)
        for s in range(STRIPS):
            tile = jnp.where(row8 == s, dest[r, s] * STRIPS + slot[r, s], tile)
        code[r][mine[r]] = tile
    label_got[member] = pltpu.roll(labels[...], lax.rem(member, 8) * PIECES, 1)
    pl.semaphore_wait(barrier, slabs + tiles - 2)

    for r in range(2):
        for peer in peers[r]:
            pltpu.make_async_remote_copy(
                src_ref=code[r].at[mine[r]], dst_ref=code[r].at[mine[r]],
                send_sem=send_sem.at[r], recv_sem=code_sem.at[r],
                device_id={axes[r]: peer}, device_id_type=MESH,
            ).start()

    def spread_start(r, i):
        peer = peers[r][i]
        pltpu.make_async_remote_copy(
            src_ref=moving.at[r, :, pl.ds(pl.multiple_of(peer * rows[r], rows[r]), rows[r]), :],
            dst_ref=got[r].at[pl.ds(mine[r] * STRIPS, STRIPS)],
            send_sem=send_sem.at[2 + r], recv_sem=spread_sem.at[r],
            device_id={axes[r]: peer}, device_id_type=MESH,
        ).start()

    for i in range(slabs - 1):
        spread_start(0, i)
        if i % 2 == 0 and i // 2 < tiles - 1:
            spread_start(1, i // 2)
    own = [
        pltpu.make_async_copy(
            moving.at[r, :, pl.ds(pl.multiple_of(mine[r] * rows[r], rows[r]), rows[r]), :],
            got[r].at[pl.ds(mine[r] * STRIPS, STRIPS)], own_sem.at[r])
        for r in range(2)
    ]
    load_fixed = pltpu.make_async_copy(fixed_in, fixed, own_sem.at[2])
    load_table = pltpu.make_async_copy(table_in, table, own_sem.at[3])
    load_fixed.start()
    load_table.start()
    for copy in own:
        copy.start()
    for peer in peers[0]:
        pl.semaphore_signal(ready, inc=1, device_id={"slab": peer}, device_id_type=MESH)

    for r in range(2):
        local_wait(code[r].at[pl.ds(0, sizes[r] - 1)], code_sem.at[r])
        total = jnp.zeros((8, W), jnp.int32)
        for i in range(sizes[r]):
            total += jnp.where(code[r][i] == lane8, i * STRIPS + row8, 0)
        source = jnp.minimum(jnp.sum(total, 0, keepdims=True), sizes[r] * STRIPS - 1)
        inv_v[r] = jnp.broadcast_to(source, (8, W))
    to_scalars = pltpu.make_async_copy(inv_v, inv_s, own_sem.at[4])
    to_scalars.start()

    pl.semaphore_wait(ready, slabs - 1)
    group_base = (p // (BAND // tiles)) * (BAND // tiles)

    def group_peer(step):
        peer = lax.rem(member + step, BAND)
        return peer, (group_base + peer // tiles, lax.rem(peer, tiles))

    def send_label(step, carry):
        pltpu.make_async_remote_copy(
            src_ref=label_got.at[member], dst_ref=label_got.at[member],
            send_sem=send_sem.at[4], recv_sem=label_sem,
            device_id=group_peer(step)[1], device_id_type=MESH,
        ).start()
        return carry

    lax.fori_loop(1, BAND, send_label, 0)

    load_fixed.wait()
    load_table.wait()

    def fixed_pair(i, carry):
        spectra = forward_pair(table, fixed[2 * i], fixed[2 * i + 1])
        fixed_spec[2 * i] = spectra[:SPEC]
        fixed_spec[2 * i + 1] = spectra[SPEC:]
        return carry

    lax.fori_loop(0, STRIPS // 2, fixed_pair, 0)

    local_wait(label_got.at[pl.ds(0, BAND - 1)], label_sem)
    columns = []
    for g in range(BAND // 8):
        total = label_got[8 * g]
        for d in range(1, 8):
            total = total + label_got[8 * g + d]
        columns.append(total)
    chunk = 256
    for s in range(STRIPS):
        def build(i, carry):
            for g in range(BAND // 8):
                want = lax.broadcasted_iota(jnp.int32, (chunk, W), 0) + i * chunk
                hit = jnp.broadcast_to(columns[g][s : s + 1], (chunk, W)) == want
                onehot[s, pl.ds(pl.multiple_of(i * chunk, chunk), chunk), W * g : W * (g + 1)] = (
                    jnp.where(hit, 1.0, 0.0).astype(BF16))
            return carry

        lax.fori_loop(0, devices * OWNED // chunk, build, 0)

    to_scalars.wait()
    for r in (1, 0):
        own[r].wait()
        local_wait(got[r].at[pl.ds(0, (sizes[r] - 1) * STRIPS)], spread_sem.at[r])

    def choose(s, carry):
        for r in (0, 1):
            place = pl.ds(pl.multiple_of(mine[r] * rows[r], rows[r]), rows[r])
            partner[r, s, place, :] = got[r][inv_s[r, 0, mine[r] * STRIPS + s]]
            for peer in peers[r]:
                pick[r][s, peer] = got[r][inv_s[r, 0, peer * STRIPS + s]]
        for r in (0, 1):
            place = pl.ds(pl.multiple_of(mine[r] * rows[r], rows[r]), rows[r])
            for peer in peers[r]:
                pltpu.make_async_remote_copy(
                    src_ref=pick[r].at[s, peer], dst_ref=partner.at[r, s, place, :],
                    send_sem=send_sem.at[5 + r], recv_sem=slot_sem.at[r, s],
                    device_id={axes[r]: peer}, device_id_type=MESH,
                ).start()
        return carry

    lax.fori_loop(0, STRIPS, choose, 0)

    def correlate(s, found):
        for r in range(2):
            local_wait(partner.at[r, s, pl.ds(0, H - rows[r])], slot_sem.at[r, s])
        spectra = forward_pair(table, partner[0, s], partner[1, s])
        surface = surfaces(table, fixed_spec[s], spectra)
        is_live = s < live[0]
        total = jnp.ones((1, 1), F32)
        acc = fixed[s]
        for r in range(2):
            peak = jnp.max(surface[:, W * r : W * (r + 1)], axis=(0, 1), keepdims=True)
            weight = 1.0 / (1.0 + jnp.exp(4.0 - peak))
            down = lax.rem(shifts[r, 0, s] + H, H)
            side = lax.rem(shifts[r, 1, s] + W, W)
            moved = pltpu.roll(pltpu.roll(partner[r, s], side, 1), down, 0)
            acc = acc + weight * moved
            total = total + weight
            shown = jnp.where(is_live, peak, 0.0)
            found = jnp.where((row8 == r) & (lane8 == s), shown, found)
        acc = jnp.where(is_live, acc * (1.0 / total), 0.0)
        for k in range(PIECES):
            merged[pl.ds(k * PAD, BAND), :] = acc[k * BAND : (k + 1) * BAND]
        here = pl.ds(pl.multiple_of(s * PIECES, PIECES), PIECES)
        for r in range(BAND):
            spread[s, r] = merged[pl.ds(r, PIECES, stride=PAD), :]
        rows_got[s, member] = spread[s, member]

        def send_rows(step, carry):
            peer, device = group_peer(step)
            pltpu.make_async_remote_copy(
                src_ref=spread.at[s, peer], dst_ref=rows_got.at[s, member],
                send_sem=send_sem.at[7], recv_sem=rows_sem.at[s],
                device_id=device, device_id_type=MESH,
            ).start()
            return carry

        lax.fori_loop(1, BAND, send_rows, 0)
        return found

    found = lax.fori_loop(0, STRIPS, correlate, jnp.zeros((8, W), F32))
    peaks[...] = found[:2, :STRIPS]

    for s in range(STRIPS):
        local_wait(rows_got.at[s, pl.ds(0, BAND - 1)], rows_sem.at[s])
        high, low = split(rows_got[s].reshape(BAND * PIECES, W))
        both = jnp.concatenate([high, low], 1)

        def add(i, carry):
            at = pl.ds(pl.multiple_of(i * chunk, chunk), chunk)
            parts = dot(onehot[s, at, :], both)
            part_sum = (parts[:, :W] + parts[:, W:]).reshape(chunk // OWNED, OWNED, W)
            owners = pl.ds(i * (chunk // OWNED), chunk // OWNED)
            if s == 0:
                sums[owners] = part_sum
            else:
                sums[owners] += part_sum
            return carry

        lax.fori_loop(0, devices * OWNED // chunk, add, 0)

    def send_owner(k, carry):
        oz = lax.rem(z + 2 + k // 32, RING)
        ox = lax.rem(x + 2 + lax.rem(k // 8, RING), RING)
        oy = lax.rem(y + 2 + lax.rem(k // 2, RING), RING)
        oc = lax.rem(c + lax.rem(k, 2), 2)
        op, oq = oz * RING + ox, oy * 2 + oc
        pltpu.make_async_remote_copy(
            src_ref=sums.at[op * tiles + oq], dst_ref=owned.at[me],
            send_sem=send_sem.at[8], recv_sem=owner_sem,
            device_id=(op, oq), device_id_type=MESH,
        ).start()
        return carry

    self_at = 2 * 32 + 2 * 8 + 2 * 2
    lax.fori_loop(0, self_at, send_owner, 0)
    lax.fori_loop(self_at + 1, devices, send_owner, 0)
    owned[me] = sums[me]

    for r in range(2):
        local_wait(code[r].at[pl.ds(0, sizes[r] - 1)], send_sem.at[r])
        local_wait(got[r].at[pl.ds(0, (sizes[r] - 1) * STRIPS)], send_sem.at[2 + r])
        local_wait(pick[r].at[:, pl.ds(0, sizes[r] - 1)], send_sem.at[5 + r])
    local_wait(label_got.at[pl.ds(0, BAND - 1)], send_sem.at[4])
    local_wait(spread.at[:, pl.ds(0, BAND - 1)], send_sem.at[7])

    local_wait(owned.at[pl.ds(0, devices - 1)], owner_sem)
    for r in range(BAND):
        total = owned[r]
        for k in range(1, devices // BAND):
            total = total + owned[k * BAND + r]
        out[:, r, :] = total
    local_wait(sums.at[pl.ds(0, devices - 1)], send_sem.at[8])


def local(slabs, tiles, fixed, moving, pair_dest, pair_slot, plane_shift, live_count, piece_block):
    table = tables()
    devices = slabs * tiles
    labels = jnp.pad(piece_block.reshape(STRIPS, PIECES), ((0, 8 - STRIPS), (0, W - PIECES)))
    smem = pl.BlockSpec(memory_space=pltpu.SMEM)
    vmem = pl.BlockSpec(memory_space=pltpu.VMEM)
    anywhere = pl.BlockSpec(memory_space=pl.ANY)
    dma = pltpu.SemaphoreType.DMA
    return pl.pallas_call(
        functools.partial(whole_kernel, slabs, tiles),
        out_shape=(
            jax.ShapeDtypeStruct((2, STRIPS), F32),
            jax.ShapeDtypeStruct((OWNED, BAND, W), F32),
        ),
        in_specs=[smem, smem, smem, smem, vmem, anywhere, anywhere, anywhere],
        out_specs=(vmem, vmem),
        scratch_shapes=[
            pltpu.VMEM((STRIPS, H, W), F32),
            pltpu.VMEM((2, TABLE_ROWS, HALF), BF16),
            pltpu.VMEM((slabs * STRIPS, H // slabs, W), F32),
            pltpu.VMEM((tiles * STRIPS, H // tiles, W), F32),
            pltpu.VMEM((STRIPS, slabs, H // slabs, W), F32),
            pltpu.VMEM((STRIPS, tiles, H // tiles, W), F32),
            pltpu.VMEM((2, STRIPS, H, W), F32),
            pltpu.VMEM((slabs, 8, W), jnp.int32),
            pltpu.VMEM((tiles, 8, W), jnp.int32),
            pltpu.VMEM((2, 8, W), jnp.int32),
            pltpu.SMEM((2, 8, W), jnp.int32),
            pltpu.VMEM((STRIPS, SPEC, 2 * W), F32),
            pltpu.VMEM((PIECES * PAD, W), F32),
            pltpu.VMEM((STRIPS, BAND, PIECES, W), F32),
            pltpu.VMEM((STRIPS, BAND, PIECES, W), F32),
            pltpu.VMEM((BAND, 8, W), jnp.int32),
            pltpu.VMEM((STRIPS, devices * OWNED, BAND * PIECES), BF16),
            pltpu.VMEM((devices, OWNED, W), F32),
            pltpu.VMEM((devices, OWNED, W), F32),
            dma((9,)), dma((2,)), dma((2,)), dma, dma((2, STRIPS)), dma((STRIPS,)), dma((5,)), dma,
            pltpu.SemaphoreType.REGULAR,
        ],
        compiler_params=pltpu.CompilerParams(
            collective_id=0, has_side_effects=True, vmem_limit_bytes=60 * 1024 * 1024
        ),
        name="register_merge",
    )(pair_dest, pair_slot, plane_shift, live_count, labels, moving, fixed, table)


def solution(mesh):
    both = ("slab", "tile")
    placed = (
        P(both, None, None),
        P(None, both, None, None),
        P(None, both),
        P(None, both),
        P(None, None, both),
        P(both),
        P(both),
    )
    return jax.shard_map(
        functools.partial(local, mesh.shape["slab"], mesh.shape["tile"]),
        mesh=mesh,
        in_specs=placed,
        out_specs=(P(None, both), P(both, None, None)),
        check_vma=False,
    )
```

time: 383 us -> 80.2 us (0.21); the launches traced: 377 us -> 80 us
  waiting for transfers between devices: 158 us -> 0 us
  Pallas kernels: 0 us -> 74.5 us
  local copies, waits for them, and re-layouts: 71.7 us -> 4.24 us
  matrix products: 58.3 us -> 0 us
  other arithmetic: 44.3 us -> 0 us
  starting transfers between devices: 42.6 us -> 0 us
    all_to_all x6 -> x0, waiting for transfers between devices: 158 us -> none  [the longest x1 68.9 us: local(): lax.all_to_all(first_send, 'slab', split_axis=0, concat_axis=0, tiled=True)]
    pallas_call x0 -> x1, Pallas kernels: none -> 74.5 us  [local(): pl.pallas_call(functools.partial(whole_kernel, slabs, tiles), out_shape=(...]
    dot_general x11 -> x0, matrix products: 58.3 us -> none  [the longest x3 17.1 us: forward(): halves = jnp.einsum('rk,bkc->brc', stacked, planes, precision=HIGHEST)]
    all_to_all x6 -> x0, starting transfers between devices: 42.6 us -> none  [the longest x2 17.8 us: one_exchange(): lax.all_to_all(blocks, axis, split_axis=0, concat_axis=0, tiled=True)]
    gather x17 -> x0, local copies, waits for them, and re-layouts: 41.3 us -> none  [the longest x6 20.2 us: shift_planes(): jnp.roll(plane, (first_shift, second_shift), axis=(0, 1))]
    select_n x17 -> x0, other arithmetic: 19.4 us -> none  [the longest x3 17.1 us: pack(): jnp.where(filled.reshape((-1,) + (1,) * (values.ndim - 1)), gathered, 0.0)]
    concatenate x4 -> x0, local copies, waits for them, and re-layouts: 8.45 us -> none  [shift_planes(): jnp.roll(plane, (first_shift, second_shift), axis=(0, 1))]
    unnamed x30 -> x2, local copies, waits for them, and re-layouts: 11.2 us -> 2.9 us
  transfers between devices with their start and end apart: 6 -> 0, of which waited for: 4 -> 0; matrix products, arithmetic and copies ran while one was open for 40% -> 0% of each run, Pallas kernels for 0% -> 0%
where the time goes in v2:
time: 80.2 us; the launch traced here: 80 us
  Pallas kernels  74.5 us (93%)
  local copies, waits for them, and re-layouts  4.24 us (5%)
  between operations  1.29 us (2%)
    pallas_call x1, Pallas kernels, local(): pl.pallas_call(functools.partial(whole_kernel, slabs, tiles), out_shape=(...  74.5 us
    unnamed x2, local copies, waits for them, and re-layouts  2.9 us

profile of v2, /device:TPU:1, one launch (start us, length us, event | category | flops | bytes accessed | tf_op | source)
XLA Modules:
  0.0 80.0 jit_solution(15614488132039532036)
XLA Ops:
  1.3 0.7 reshape.7
  2.0 0.6 pad.4.labels
  2.6 74.5 %register_merge.1 = (f32[2,4]{1,0:T(2,128)}, f32[16,32,128]{2,1,0:T(8,128)}) custom-call(s32[2,4]{1,0:T(2,128)} %dest.1, s32[2,4]{1,0:T(2,128)} %slot.1, s32[2,2,4]{2,1,0:T(2,128)} %shifts.1, s32[1]{0:T(128)S(6)} %copy.12.live, s32[8,128]{1,0:T(8,128)} %pad.4.labels, f32[2,4,512,128]{3,2,1,0:T(8,128)} %moving.1, f32[4,512,128]{2,1,0:T(8,128)} %fixed_in.1, ...), custom_call_target="tpu_custom_call" | custom-call | tf_op jit(solution)/shard_map/register_merge/pallas_call | solution.py:411
  77.1 1.2 %copy.13 = f32[2,4]{1,0:T(2,128)} copy(f32[2,4]{1,0:T(2,128)} %get-tuple-element.4) | data formatting | bytes 64
  78.3 1.7 %copy.14 = f32[16,32,128]{2,1,0:T(8,128)} copy(f32[16,32,128]{2,1,0:T(8,128)} %get-tuple-element.5) | data formatting | bytes 524288

commit v3 on v2

--- a/solution.py
+++ b/solution.py
@@ -24,6 +24,9 @@
 SPEC = HALF + 8
 PAD = BAND + 8
 RING = 4
+GROUP = 2 * BAND
+HALF_LANES = W // 2
+SHARE = PIECES // 2
 FIRST = HALF + 16
 
 
@@ -142,9 +145,9 @@
 
 
 def whole_kernel(
-    slabs, tiles, dest, slot, shifts, live, labels, moving, fixed_in, table_in, peaks, out,
-    fixed, table, got0, got1, pick0, pick1, partner, code0, code1, inv_v, inv_s, fixed_spec,
-    merged, spread, rows_got, label_got, onehot, sums, owned,
+    slabs, tiles, dest_in, slot_in, shifts_in, live, block_in, moving, fixed_in, table_in,
+    peaks, owned, dest, slot, shifts, block, fixed, table, got0, got1, pick0, pick1, partner, code0, code1, inv_v, inv_s, fixed_spec,
+    merged, spread, rows_got, label_got, onehot, sums, packed,
     send_sem, spread_sem, code_sem, label_sem, slot_sem, rows_sem, own_sem, owner_sem, ready,
 ):
     p = lax.axis_index("slab")
@@ -152,7 +155,7 @@
     z, x = p // RING, lax.rem(p, RING)
     y, c = q // 2, lax.rem(q, 2)
     me = p * tiles + q
-    member = lax.rem(me, BAND)
+    member = lax.rem(me, GROUP)
     devices = slabs * tiles
     axes = ("slab", "tile")
     sizes = (slabs, tiles)
@@ -183,12 +186,26 @@
     for r in range(2):
         for peer in peers[r]:
             pl.semaphore_signal(barrier, inc=1, device_id={axes[r]: peer}, device_id_type=MESH)
+    small = [
+        pltpu.make_async_copy(a, b, own_sem.at[5 + i])
+        for i, (a, b) in enumerate((
+            (dest_in, dest), (slot_in, slot), (shifts_in, shifts), (block_in, block)))
+    ]
+    for copy in small:
+        copy.start()
+    for copy in small:
+        copy.wait()
     for r in range(2):
         tile = jnp.full((8, W), -1, jnp.int32)
         for s in range(STRIPS):
             tile = jnp.where(row8 == s, dest[r, s] * STRIPS + slot[r, s], tile)
         code[r][mine[r]] = tile
-    label_got[member] = pltpu.roll(labels[...], lax.rem(member, 8) * PIECES, 1)
+    tile = jnp.zeros((8, W), jnp.int32)
+    for s in range(STRIPS):
+        for k in range(PIECES):
+            at = (row8 == (k // SHARE) * STRIPS + s) & (lane8 == k % SHARE)
+            tile = jnp.where(at, block[s * PIECES + k], tile)
+    label_got[member] = pltpu.roll(tile, lax.rem(member, W // SHARE) * SHARE, 1)
     pl.semaphore_wait(barrier, slabs + tiles - 2)
 
     for r in range(2):
@@ -238,10 +255,10 @@
     to_scalars.start()
 
     pl.semaphore_wait(ready, slabs - 1)
-    group_base = (p // (BAND // tiles)) * (BAND // tiles)
+    group_base = (p // (GROUP // tiles)) * (GROUP // tiles)
 
     def group_peer(step):
-        peer = lax.rem(member + step, BAND)
+        peer = lax.rem(member + step, GROUP)
         return peer, (group_base + peer // tiles, lax.rem(peer, tiles))
 
     def send_label(step, carry):
@@ -252,7 +269,7 @@
         ).start()
         return carry
 
-    lax.fori_loop(1, BAND, send_label, 0)
+    lax.fori_loop(1, GROUP, send_label, 0)
 
     load_fixed.wait()
     load_table.wait()
@@ -265,24 +282,31 @@
 
     lax.fori_loop(0, STRIPS // 2, fixed_pair, 0)
 
-    local_wait(label_got.at[pl.ds(0, BAND - 1)], label_sem)
+    local_wait(label_got.at[pl.ds(0, GROUP - 1)], label_sem)
     columns = []
-    for g in range(BAND // 8):
-        total = label_got[8 * g]
-        for d in range(1, 8):
-            total = total + label_got[8 * g + d]
+    for g in range(GROUP * SHARE // W):
+        total = label_got[W // SHARE * g]
+        for d in range(1, W // SHARE):
+            total = total + label_got[W // SHARE * g + d]
         columns.append(total)
     chunk = 256
-    for s in range(STRIPS):
+
+    def build_slot(s):
         def build(i, carry):
-            for g in range(BAND // 8):
-                want = lax.broadcasted_iota(jnp.int32, (chunk, W), 0) + i * chunk
-                hit = jnp.broadcast_to(columns[g][s : s + 1], (chunk, W)) == want
-                onehot[s, pl.ds(pl.multiple_of(i * chunk, chunk), chunk), W * g : W * (g + 1)] = (
-                    jnp.where(hit, 1.0, 0.0).astype(BF16))
+            want = lax.broadcasted_iota(jnp.int32, (chunk, W), 0) + i * chunk
+            for half in range(2):
+                for g, column in enumerate(columns):
+                    at = half * STRIPS + s
+                    hit = jnp.broadcast_to(column[at : at + 1], (chunk, W)) == want
+                    lanes = W * (len(columns) * half + g)
+                    onehot[s, pl.ds(pl.multiple_of(i * chunk, chunk), chunk), lanes : lanes + W] = (
+                        jnp.where(hit, 1.0, 0.0).astype(BF16))
             return carry
 
         lax.fori_loop(0, devices * OWNED // chunk, build, 0)
+
+    build_slot(0)
+    build_slot(1)
 
     to_scalars.wait()
     for r in (1, 0):
@@ -306,6 +330,11 @@
         return carry
 
     lax.fori_loop(0, STRIPS, choose, 0)
+
+    build_slot(2)
+    build_slot(3)
+
+    low_half = lane8 < HALF_LANES
 
     def correlate(s, found):
         for r in range(2):
@@ -328,9 +357,11 @@
         acc = jnp.where(is_live, acc * (1.0 / total), 0.0)
         for k in range(PIECES):
             merged[pl.ds(k * PAD, BAND), :] = acc[k * BAND : (k + 1) * BAND]
-        here = pl.ds(pl.multiple_of(s * PIECES, PIECES), PIECES)
         for r in range(BAND):
-            spread[s, r] = merged[pl.ds(r, PIECES, stride=PAD), :]
+            top = merged[pl.ds(r, SHARE, stride=PAD), :]
+            bottom = merged[pl.ds(r + SHARE * PAD, SHARE, stride=PAD), :]
+            spread[s, 2 * r] = jnp.where(low_half, top, pltpu.roll(bottom, HALF_LANES, 1))
+            spread[s, 2 * r + 1] = jnp.where(low_half, pltpu.roll(top, HALF_LANES, 1), bottom)
         rows_got[s, member] = spread[s, member]
 
         def send_rows(step, carry):
@@ -342,29 +373,38 @@
             ).start()
             return carry
 
-        lax.fori_loop(1, BAND, send_rows, 0)
+        lax.fori_loop(1, GROUP, send_rows, 0)
         return found
 
     found = lax.fori_loop(0, STRIPS, correlate, jnp.zeros((8, W), F32))
-    peaks[...] = found[:2, :STRIPS]
-
+    peaks[...] = found
+
+    big = 1024
+    low_rows = lax.broadcasted_iota(jnp.int32, (GROUP * SHARE, W), 1) < HALF_LANES
     for s in range(STRIPS):
-        local_wait(rows_got.at[s, pl.ds(0, BAND - 1)], rows_sem.at[s])
-        high, low = split(rows_got[s].reshape(BAND * PIECES, W))
-        both = jnp.concatenate([high, low], 1)
+        local_wait(rows_got.at[s, pl.ds(0, GROUP - 1)], rows_sem.at[s])
+        rows_here = rows_got[s].reshape(GROUP * SHARE, W)
+        high = rows_here.astype(BF16).astype(F32)
+        low = rows_here - high
+        both = jnp.concatenate([
+            jnp.where(low_rows, high, pltpu.roll(low, HALF_LANES, 1)),
+            jnp.where(low_rows, pltpu.roll(high, HALF_LANES, 1), low),
+        ], 0).astype(BF16)
 
         def add(i, carry):
-            at = pl.ds(pl.multiple_of(i * chunk, chunk), chunk)
-            parts = dot(onehot[s, at, :], both)
-            part_sum = (parts[:, :W] + parts[:, W:]).reshape(chunk // OWNED, OWNED, W)
-            owners = pl.ds(i * (chunk // OWNED), chunk // OWNED)
-            if s == 0:
-                sums[owners] = part_sum
+            at = pl.ds(pl.multiple_of(i * big, big), big)
+            total = dot(onehot[s, at, :], both)
+            if s > 0:
+                total = total + sums[at, :]
+            if s < STRIPS - 1:
+                sums[at, :] = total
             else:
-                sums[owners] += part_sum
+                total = (total + pltpu.roll(total, HALF_LANES, 1)).reshape(big // OWNED, 2, 8, W)
+                owners = pl.ds(i * (big // OWNED), big // OWNED)
+                packed[owners] = jnp.where(low_half[None], total[:, 0], total[:, 1])
             return carry
 
-        lax.fori_loop(0, devices * OWNED // chunk, add, 0)
+        lax.fori_loop(0, devices * OWNED // big, add, 0)
 
     def send_owner(k, carry):
         oz = lax.rem(z + 2 + k // 32, RING)
@@ -373,7 +413,7 @@
         oc = lax.rem(c + lax.rem(k, 2), 2)
         op, oq = oz * RING + ox, oy * 2 + oc
         pltpu.make_async_remote_copy(
-            src_ref=sums.at[op * tiles + oq], dst_ref=owned.at[me],
+            src_ref=packed.at[op * tiles + oq], dst_ref=owned.at[me],
             send_sem=send_sem.at[8], recv_sem=owner_sem,
             device_id=(op, oq), device_id_type=MESH,
         ).start()
@@ -382,41 +422,50 @@
     self_at = 2 * 32 + 2 * 8 + 2 * 2
     lax.fori_loop(0, self_at, send_owner, 0)
     lax.fori_loop(self_at + 1, devices, send_owner, 0)
-    owned[me] = sums[me]
+    last = pltpu.make_async_copy(packed.at[me], owned.at[me], own_sem.at[4])
+    last.start()
 
     for r in range(2):
         local_wait(code[r].at[pl.ds(0, sizes[r] - 1)], send_sem.at[r])
         local_wait(got[r].at[pl.ds(0, (sizes[r] - 1) * STRIPS)], send_sem.at[2 + r])
         local_wait(pick[r].at[:, pl.ds(0, sizes[r] - 1)], send_sem.at[5 + r])
-    local_wait(label_got.at[pl.ds(0, BAND - 1)], send_sem.at[4])
-    local_wait(spread.at[:, pl.ds(0, BAND - 1)], send_sem.at[7])
-
-    local_wait(owned.at[pl.ds(0, devices - 1)], owner_sem)
+    local_wait(label_got.at[pl.ds(0, GROUP - 1)], send_sem.at[4])
+    local_wait(spread.at[:, pl.ds(0, GROUP - 1)], send_sem.at[7])
+
+    last.wait()
+    local_wait(packed.at[pl.ds(0, devices - 1)], owner_sem)
+    local_wait(packed.at[pl.ds(0, devices - 1)], send_sem.at[8])
+
+
+def finish_kernel(found, owned, peaks, out):
+    peaks[...] = found[:2, :STRIPS]
+    low_half = lax.broadcasted_iota(jnp.int32, (8, W), 1) < HALF_LANES
     for r in range(BAND):
-        total = owned[r]
-        for k in range(1, devices // BAND):
-            total = total + owned[k * BAND + r]
-        out[:, r, :] = total
-    local_wait(sums.at[pl.ds(0, devices - 1)], send_sem.at[8])
+        a, b = owned[2 * r], owned[2 * r + 1]
+        for k in range(1, owned.shape[0] // GROUP):
+            a = a + owned[k * GROUP + 2 * r]
+            b = b + owned[k * GROUP + 2 * r + 1]
+        out[:8, r, :] = jnp.where(low_half, a, pltpu.roll(b, HALF_LANES, 1))
+        out[8:, r, :] = jnp.where(low_half, pltpu.roll(a, HALF_LANES, 1), b)
 
 
 def local(slabs, tiles, fixed, moving, pair_dest, pair_slot, plane_shift, live_count, piece_block):
     table = tables()
     devices = slabs * tiles
-    labels = jnp.pad(piece_block.reshape(STRIPS, PIECES), ((0, 8 - STRIPS), (0, W - PIECES)))
-    smem = pl.BlockSpec(memory_space=pltpu.SMEM)
     vmem = pl.BlockSpec(memory_space=pltpu.VMEM)
     anywhere = pl.BlockSpec(memory_space=pl.ANY)
     dma = pltpu.SemaphoreType.DMA
-    return pl.pallas_call(
+    small = (pair_dest, pair_slot, plane_shift, live_count, piece_block)
+    found, owned = pl.pallas_call(
         functools.partial(whole_kernel, slabs, tiles),
         out_shape=(
-            jax.ShapeDtypeStruct((2, STRIPS), F32),
-            jax.ShapeDtypeStruct((OWNED, BAND, W), F32),
+            jax.ShapeDtypeStruct((8, W), F32),
+            jax.ShapeDtypeStruct((devices, 8, W), F32),
         ),
-        in_specs=[smem, smem, smem, smem, vmem, anywhere, anywhere, anywhere],
-        out_specs=(vmem, vmem),
-        scratch_shapes=[
+        in_specs=[anywhere] * 3 + [pl.BlockSpec(memory_space=pltpu.SMEM)] + [anywhere] * 4,
+        out_specs=(vmem, anywhere),
+        scratch_shapes=[pltpu.SMEM(a.shape, jnp.int32) for a in small if a.shape != (1,)]
+        + [
             pltpu.VMEM((STRIPS, H, W), F32),
             pltpu.VMEM((2, TABLE_ROWS, HALF), BF16),
             pltpu.VMEM((slabs * STRIPS, H // slabs, W), F32),
@@ -430,20 +479,30 @@
             pltpu.SMEM((2, 8, W), jnp.int32),
             pltpu.VMEM((STRIPS, SPEC, 2 * W), F32),
             pltpu.VMEM((PIECES * PAD, W), F32),
-            pltpu.VMEM((STRIPS, BAND, PIECES, W), F32),
-            pltpu.VMEM((STRIPS, BAND, PIECES, W), F32),
-            pltpu.VMEM((BAND, 8, W), jnp.int32),
-            pltpu.VMEM((STRIPS, devices * OWNED, BAND * PIECES), BF16),
-            pltpu.VMEM((devices, OWNED, W), F32),
-            pltpu.VMEM((devices, OWNED, W), F32),
-            dma((9,)), dma((2,)), dma((2,)), dma, dma((2, STRIPS)), dma((STRIPS,)), dma((5,)), dma,
+            pltpu.VMEM((STRIPS, GROUP, SHARE, W), F32),
+            pltpu.VMEM((STRIPS, GROUP, SHARE, W), F32),
+            pltpu.VMEM((GROUP, 8, W), jnp.int32),
+            pltpu.VMEM((STRIPS, devices * OWNED, GROUP * PIECES), BF16),
+            pltpu.VMEM((devices * OWNED, W), F32),
+            pltpu.VMEM((devices, 8, W), F32),
+            dma((9,)), dma((2,)), dma((2,)), dma, dma((2, STRIPS)), dma((STRIPS,)), dma((10,)), dma,
             pltpu.SemaphoreType.REGULAR,
         ],
         compiler_params=pltpu.CompilerParams(
             collective_id=0, has_side_effects=True, vmem_limit_bytes=60 * 1024 * 1024
         ),
         name="register_merge",
-    )(pair_dest, pair_slot, plane_shift, live_count, labels, moving, fixed, table)
+    )(*small, moving, fixed, table)
+    return pl.pallas_call(
+        finish_kernel,
+        out_shape=(
+            jax.ShapeDtypeStruct((2, STRIPS), F32),
+            jax.ShapeDtypeStruct((OWNED, BAND, W), F32),
+        ),
+        in_specs=[vmem, vmem],
+        out_specs=(vmem, vmem),
+        name="finish_blocks",
+    )(found, owned)
 
 
 def solution(mesh):

time: 80.2 us -> 72.8 us (0.908)
  local copies, waits for them, and re-layouts: 4.24 us -> 0 us
  Pallas kernels: 74.5 us -> 71.3 us
    pallas_call x1, Pallas kernels: 74.5 us -> 69.3 us  [local(): pl.pallas_call(functools.partial(whole_kernel, slabs, tiles), out_shape=(...]
    unnamed x2 -> x0, local copies, waits for them, and re-layouts: 2.9 us -> none
    pallas_call x0 -> x1, Pallas kernels: none -> 2.02 us  [local(): pl.pallas_call(finish_kernel, out_shape=(jax.ShapeDtypeStruct((2, STRIPS)...]
where the time goes in v3:
time: 72.8 us; the launch traced here: 72.6 us
  Pallas kernels  71.3 us (98%)
  between operations  1.29 us (2%)
    pallas_call x1, Pallas kernels, local(): pl.pallas_call(functools.partial(whole_kernel, slabs, tiles), out_shape=(...  69.3 us
    pallas_call x1, Pallas kernels, local(): pl.pallas_call(finish_kernel, out_shape=(jax.ShapeDtypeStruct((2, STRIPS)...  2.02 us

profile of v3, /device:TPU:1, one launch (start us, length us, event | category | flops | bytes accessed | tf_op | source)
XLA Modules:
  0.0 72.6 jit_solution(2117095597151414499)
XLA Ops:
  1.3 69.3 %register_merge.1 = (f32[8,128]{1,0:T(8,128)}, f32[128,8,128]{2,1,0:T(8,128)}) custom-call(s32[2,4]{1,0:T(2,128)} %dest_in.1, s32[2,4]{1,0:T(2,128)} %slot_in.1, s32[2,2,4]{2,1,0:T(2,128)} %shifts_in.1, s32[1]{0:T(128)S(6)} %copy.10.live, s32[64]{0:T(128)} %block_in.1, f32[2,4,512,128]{3,2,1,0:T(8,128)} %moving.1, f32[4,512,128]{2,1,0:T(8,128)} %fixed_in.1, ...), custom_call_target="tpu_custom_call" | custom-call | tf_op jit(solution)/shard_map/register_merge/pallas_call | solution.py:459
  70.6 2.0 %finish_blocks.1 = (f32[2,4]{1,0:T(2,128)}, f32[16,32,128]{2,1,0:T(8,128)}) custom-call(f32[8,128]{1,0:T(8,128)} %get-tuple-element.4.found, f32[128,8,128]{2,1,0:T(8,128)} %get-tuple-element.5.owned), custom_call_target="tpu_custom_call" | custom-call | tf_op jit(solution)/shard_map/finish_blocks/pallas_call | solution.py:496

commit v4 on v3

--- a/solution.py
+++ b/solution.py
@@ -146,7 +146,7 @@
 
 def whole_kernel(
     slabs, tiles, dest_in, slot_in, shifts_in, live, block_in, moving, fixed_in, table_in,
-    peaks, owned, dest, slot, shifts, block, fixed, table, got0, got1, pick0, pick1, partner, code0, code1, inv_v, inv_s, fixed_spec,
+    peaks, owned, dest, slot, shifts, block, fixed, table, got00, got01, got10, got11, pick0, pick1, partner, code0, code1, inv_v, inv_s, fixed_spec,
     merged, spread, rows_got, label_got, onehot, sums, packed,
     send_sem, spread_sem, code_sem, label_sem, slot_sem, rows_sem, own_sem, owner_sem, ready,
 ):
@@ -160,7 +160,7 @@
     axes = ("slab", "tile")
     sizes = (slabs, tiles)
     mine = (p, q)
-    got = (got0, got1)
+    got = ((got00, got01), (got10, got11))
     pick = (pick0, pick1)
     code = (code0, code1)
     rows = (H // slabs, H // tiles)
@@ -216,30 +216,36 @@
                 device_id={axes[r]: peer}, device_id_type=MESH,
             ).start()
 
-    def spread_start(r, i):
+    def chunk_rows(r, at, half):
+        part_rows = rows[r] // 2
+        return pl.ds(pl.multiple_of(at * rows[r] + half * part_rows, part_rows), part_rows)
+
+    def spread_start(r, i, half):
         peer = peers[r][i]
         pltpu.make_async_remote_copy(
-            src_ref=moving.at[r, :, pl.ds(pl.multiple_of(peer * rows[r], rows[r]), rows[r]), :],
-            dst_ref=got[r].at[pl.ds(mine[r] * STRIPS, STRIPS)],
-            send_sem=send_sem.at[2 + r], recv_sem=spread_sem.at[r],
+            src_ref=moving.at[r, :, chunk_rows(r, peer, half), :],
+            dst_ref=got[r][half].at[pl.ds(mine[r] * STRIPS, STRIPS)],
+            send_sem=send_sem.at[2 + r], recv_sem=spread_sem.at[r, half],
             device_id={axes[r]: peer}, device_id_type=MESH,
         ).start()
 
-    for i in range(slabs - 1):
-        spread_start(0, i)
-        if i % 2 == 0 and i // 2 < tiles - 1:
-            spread_start(1, i // 2)
-    own = [
-        pltpu.make_async_copy(
-            moving.at[r, :, pl.ds(pl.multiple_of(mine[r] * rows[r], rows[r]), rows[r]), :],
-            got[r].at[pl.ds(mine[r] * STRIPS, STRIPS)], own_sem.at[r])
-        for r in range(2)
-    ]
-    load_fixed = pltpu.make_async_copy(fixed_in, fixed, own_sem.at[2])
-    load_table = pltpu.make_async_copy(table_in, table, own_sem.at[3])
+    own = []
+    for half in range(2):
+        for i in range(slabs - 1):
+            spread_start(0, i, half)
+            if i % 2 == 0 and i // 2 < tiles - 1:
+                spread_start(1, i // 2, half)
+        own.append([
+            pltpu.make_async_copy(
+                moving.at[r, :, chunk_rows(r, mine[r], half), :],
+                got[r][half].at[pl.ds(mine[r] * STRIPS, STRIPS)], own_sem.at[2 * r + half])
+            for r in range(2)
+        ])
+    load_fixed = pltpu.make_async_copy(fixed_in, fixed, own_sem.at[10])
+    load_table = pltpu.make_async_copy(table_in, table, own_sem.at[11])
     load_fixed.start()
     load_table.start()
-    for copy in own:
+    for copy in own[0] + own[1]:
         copy.start()
     for peer in peers[0]:
         pl.semaphore_signal(ready, inc=1, device_id={"slab": peer}, device_id_type=MESH)
@@ -255,21 +261,30 @@
     to_scalars.start()
 
     pl.semaphore_wait(ready, slabs - 1)
-    group_base = (p // (GROUP // tiles)) * (GROUP // tiles)
-
-    def group_peer(step):
-        peer = lax.rem(member + step, GROUP)
-        return peer, (group_base + peer // tiles, lax.rem(peer, tiles))
-
-    def send_label(step, carry):
+    group_rows = GROUP // tiles
+    group_base = (p // group_rows) * group_rows
+    tile_ring = [lax.rem(q + i, tiles) for i in range(tiles)]
+
+    def to_group(send):
+        for i in range(1, tiles):
+            send(member - q + tile_ring[i], (p, tile_ring[i]))
+
+        def row(j, carry):
+            at = lax.rem(p + j, group_rows)
+            for i in range(tiles):
+                send(at * tiles + tile_ring[i], (group_base + at, tile_ring[i]))
+            return carry
+
+        lax.fori_loop(1, group_rows, row, 0)
+
+    def send_label(peer, device):
         pltpu.make_async_remote_copy(
             src_ref=label_got.at[member], dst_ref=label_got.at[member],
             send_sem=send_sem.at[4], recv_sem=label_sem,
-            device_id=group_peer(step)[1], device_id_type=MESH,
+            device_id=device, device_id_type=MESH,
         ).start()
-        return carry
-
-    lax.fori_loop(1, GROUP, send_label, 0)
+
+    to_group(send_label)
 
     load_fixed.wait()
     load_table.wait()
@@ -309,30 +324,34 @@
     build_slot(1)
 
     to_scalars.wait()
-    for r in (1, 0):
-        own[r].wait()
-        local_wait(got[r].at[pl.ds(0, (sizes[r] - 1) * STRIPS)], spread_sem.at[r])
-
-    def choose(s, carry):
-        for r in (0, 1):
-            place = pl.ds(pl.multiple_of(mine[r] * rows[r], rows[r]), rows[r])
-            partner[r, s, place, :] = got[r][inv_s[r, 0, mine[r] * STRIPS + s]]
-            for peer in peers[r]:
-                pick[r][s, peer] = got[r][inv_s[r, 0, peer * STRIPS + s]]
-        for r in (0, 1):
-            place = pl.ds(pl.multiple_of(mine[r] * rows[r], rows[r]), rows[r])
-            for peer in peers[r]:
-                pltpu.make_async_remote_copy(
-                    src_ref=pick[r].at[s, peer], dst_ref=partner.at[r, s, place, :],
-                    send_sem=send_sem.at[5 + r], recv_sem=slot_sem.at[r, s],
-                    device_id={axes[r]: peer}, device_id_type=MESH,
-                ).start()
-        return carry
-
-    lax.fori_loop(0, STRIPS, choose, 0)
-
+
+    def second(half):
+        for r in (1, 0):
+            own[half][r].wait()
+            local_wait(got[r][half].at[pl.ds(0, (sizes[r] - 1) * STRIPS)], spread_sem.at[r, half])
+
+        def choose(s, carry):
+            for r in (0, 1):
+                place = chunk_rows(r, mine[r], half)
+                partner[r, s, place, :] = got[r][half][inv_s[r, 0, mine[r] * STRIPS + s]]
+                for peer in peers[r]:
+                    pick[r][half, s, peer] = got[r][half][inv_s[r, 0, peer * STRIPS + s]]
+            for r in (0, 1):
+                place = chunk_rows(r, mine[r], half)
+                for peer in peers[r]:
+                    pltpu.make_async_remote_copy(
+                        src_ref=pick[r].at[half, s, peer], dst_ref=partner.at[r, s, place, :],
+                        send_sem=send_sem.at[5 + r], recv_sem=slot_sem.at[r, s],
+                        device_id={axes[r]: peer}, device_id_type=MESH,
+                    ).start()
+            return carry
+
+        lax.fori_loop(0, STRIPS, choose, 0)
+
+    second(0)
     build_slot(2)
     build_slot(3)
+    second(1)
 
     low_half = lane8 < HALF_LANES
 
@@ -364,16 +383,14 @@
             spread[s, 2 * r + 1] = jnp.where(low_half, pltpu.roll(top, HALF_LANES, 1), bottom)
         rows_got[s, member] = spread[s, member]
 
-        def send_rows(step, carry):
-            peer, device = group_peer(step)
+        def send_rows(peer, device):
             pltpu.make_async_remote_copy(
                 src_ref=spread.at[s, peer], dst_ref=rows_got.at[s, member],
                 send_sem=send_sem.at[7], recv_sem=rows_sem.at[s],
                 device_id=device, device_id_type=MESH,
             ).start()
-            return carry
-
-        lax.fori_loop(1, GROUP, send_rows, 0)
+
+        to_group(send_rows)
         return found
 
     found = lax.fori_loop(0, STRIPS, correlate, jnp.zeros((8, W), F32))
@@ -406,29 +423,31 @@
 
         lax.fori_loop(0, devices * OWNED // big, add, 0)
 
-    def send_owner(k, carry):
-        oz = lax.rem(z + 2 + k // 32, RING)
-        ox = lax.rem(x + 2 + lax.rem(k // 8, RING), RING)
-        oy = lax.rem(y + 2 + lax.rem(k // 2, RING), RING)
-        oc = lax.rem(c + lax.rem(k, 2), 2)
-        op, oq = oz * RING + ox, oy * 2 + oc
+    def send_owner(op, oq):
         pltpu.make_async_remote_copy(
             src_ref=packed.at[op * tiles + oq], dst_ref=owned.at[me],
             send_sem=send_sem.at[8], recv_sem=owner_sem,
             device_id=(op, oq), device_id_type=MESH,
         ).start()
+
+    def owner_row(j, carry):
+        op = lax.rem(z + 2 + j // RING, RING) * RING + lax.rem(x + 2 + lax.rem(j, RING), RING)
+        for oq in peers[1] + [q]:
+            send_owner(op, oq)
         return carry
 
-    self_at = 2 * 32 + 2 * 8 + 2 * 2
-    lax.fori_loop(0, self_at, send_owner, 0)
-    lax.fori_loop(self_at + 1, devices, send_owner, 0)
+    own_row = 2 * RING + 2
+    lax.fori_loop(0, own_row, owner_row, 0)
+    for oq in peers[1]:
+        send_owner(p, oq)
+    lax.fori_loop(own_row + 1, slabs, owner_row, 0)
     last = pltpu.make_async_copy(packed.at[me], owned.at[me], own_sem.at[4])
     last.start()
 
     for r in range(2):
         local_wait(code[r].at[pl.ds(0, sizes[r] - 1)], send_sem.at[r])
-        local_wait(got[r].at[pl.ds(0, (sizes[r] - 1) * STRIPS)], send_sem.at[2 + r])
-        local_wait(pick[r].at[:, pl.ds(0, sizes[r] - 1)], send_sem.at[5 + r])
+        local_wait(pick[r].at[:, :, pl.ds(0, sizes[r] - 1)], send_sem.at[2 + r])
+        local_wait(pick[r].at[:, :, pl.ds(0, sizes[r] - 1)], send_sem.at[5 + r])
     local_wait(label_got.at[pl.ds(0, GROUP - 1)], send_sem.at[4])
     local_wait(spread.at[:, pl.ds(0, GROUP - 1)], send_sem.at[7])
 
@@ -468,10 +487,12 @@
         + [
             pltpu.VMEM((STRIPS, H, W), F32),
             pltpu.VMEM((2, TABLE_ROWS, HALF), BF16),
-            pltpu.VMEM((slabs * STRIPS, H // slabs, W), F32),
-            pltpu.VMEM((tiles * STRIPS, H // tiles, W), F32),
-            pltpu.VMEM((STRIPS, slabs, H // slabs, W), F32),
-            pltpu.VMEM((STRIPS, tiles, H // tiles, W), F32),
+            pltpu.VMEM((slabs * STRIPS, H // slabs // 2, W), F32),
+            pltpu.VMEM((slabs * STRIPS, H // slabs // 2, W), F32),
+            pltpu.VMEM((tiles * STRIPS, H // tiles // 2, W), F32),
+            pltpu.VMEM((tiles * STRIPS, H // tiles // 2, W), F32),
+            pltpu.VMEM((2, STRIPS, slabs, H // slabs // 2, W), F32),
+            pltpu.VMEM((2, STRIPS, tiles, H // tiles // 2, W), F32),
             pltpu.VMEM((2, STRIPS, H, W), F32),
             pltpu.VMEM((slabs, 8, W), jnp.int32),
             pltpu.VMEM((tiles, 8, W), jnp.int32),
@@ -485,7 +506,7 @@
             pltpu.VMEM((STRIPS, devices * OWNED, GROUP * PIECES), BF16),
             pltpu.VMEM((devices * OWNED, W), F32),
             pltpu.VMEM((devices, 8, W), F32),
-            dma((9,)), dma((2,)), dma((2,)), dma, dma((2, STRIPS)), dma((STRIPS,)), dma((10,)), dma,
+            dma((9,)), dma((2, 2)), dma((2,)), dma, dma((2, STRIPS)), dma((STRIPS,)), dma((12,)), dma,
             pltpu.SemaphoreType.REGULAR,
         ],
         compiler_params=pltpu.CompilerParams(

time: 72.8 us -> 73.4 us (level)
  no operation moved by 1% of the time
where the time goes in v4:
time: 73.4 us; the launch traced here: 73.2 us
  Pallas kernels  72 us (98%)
  between operations  1.29 us (2%)
    pallas_call x1, Pallas kernels, local(): pl.pallas_call(functools.partial(whole_kernel, slabs, tiles), out_shape=(...  69.9 us
    pallas_call x1, Pallas kernels, local(): pl.pallas_call(finish_kernel, out_shape=(jax.ShapeDtypeStruct((2, STRIPS)...  2.02 us

profile of v4, /device:TPU:1, one launch (start us, length us, event | category | flops | bytes accessed | tf_op | source)
XLA Modules:
  0.0 73.2 jit_solution(12365581356242049229)
XLA Ops:
  1.3 69.9 %register_merge.1 = (f32[8,128]{1,0:T(8,128)}, f32[128,8,128]{2,1,0:T(8,128)}) custom-call(s32[2,4]{1,0:T(2,128)} %dest_in.1, s32[2,4]{1,0:T(2,128)} %slot_in.1, s32[2,2,4]{2,1,0:T(2,128)} %shifts_in.1, s32[1]{0:T(128)S(6)} %copy.10.live, s32[64]{0:T(128)} %block_in.1, f32[2,4,512,128]{3,2,1,0:T(8,128)} %moving.1, f32[4,512,128]{2,1,0:T(8,128)} %fixed_in.1, ...), custom_call_target="tpu_custom_call" | custom-call | tf_op jit(solution)/shard_map/register_merge/pallas_call | solution.py:478
  71.2 2.0 %finish_blocks.1 = (f32[2,4]{1,0:T(2,128)}, f32[16,32,128]{2,1,0:T(8,128)}) custom-call(f32[8,128]{1,0:T(8,128)} %get-tuple-element.4.found, f32[128,8,128]{2,1,0:T(8,128)} %get-tuple-element.5.owned), custom_call_target="tpu_custom_call" | custom-call | tf_op jit(solution)/shard_map/finish_blocks/pallas_call | solution.py:517

commit v5 on v4

--- a/solution.py
+++ b/solution.py
@@ -27,6 +27,7 @@
 GROUP = 2 * BAND
 HALF_LANES = W // 2
 SHARE = PIECES // 2
+PARTS = 1
 FIRST = HALF + 16
 
 
@@ -131,6 +132,12 @@
     return even + jnp.abs(odd)
 
 
+def shuffled(outer, inner, whole=False):
+    pairs = [(j, i) for j in range(outer) for i in range(inner) if whole or j or i]
+    order = np.random.default_rng(7).permutation(len(pairs))
+    return [pairs[k] for k in order]
+
+
 def far_first(*sizes):
     grid = [[]]
     for size in sizes:
@@ -146,7 +153,7 @@
 
 def whole_kernel(
     slabs, tiles, dest_in, slot_in, shifts_in, live, block_in, moving, fixed_in, table_in,
-    peaks, owned, dest, slot, shifts, block, fixed, table, got00, got01, got10, got11, pick0, pick1, partner, code0, code1, inv_v, inv_s, fixed_spec,
+    peaks, owned, dest, slot, shifts, block, fixed, table, gots, pick0, pick1, partner, code0, code1, inv_v, inv_s, fixed_spec,
     merged, spread, rows_got, label_got, onehot, sums, packed,
     send_sem, spread_sem, code_sem, label_sem, slot_sem, rows_sem, own_sem, owner_sem, ready,
 ):
@@ -160,7 +167,7 @@
     axes = ("slab", "tile")
     sizes = (slabs, tiles)
     mine = (p, q)
-    got = ((got00, got01), (got10, got11))
+    got = (gots[:PARTS], gots[PARTS:])
     pick = (pick0, pick1)
     code = (code0, code1)
     rows = (H // slabs, H // tiles)
@@ -217,7 +224,7 @@
             ).start()
 
     def chunk_rows(r, at, half):
-        part_rows = rows[r] // 2
+        part_rows = rows[r] // PARTS
         return pl.ds(pl.multiple_of(at * rows[r] + half * part_rows, part_rows), part_rows)
 
     def spread_start(r, i, half):
@@ -230,7 +237,7 @@
         ).start()
 
     own = []
-    for half in range(2):
+    for half in range(PARTS):
         for i in range(slabs - 1):
             spread_start(0, i, half)
             if i % 2 == 0 and i // 2 < tiles - 1:
@@ -238,15 +245,16 @@
         own.append([
             pltpu.make_async_copy(
                 moving.at[r, :, chunk_rows(r, mine[r], half), :],
-                got[r][half].at[pl.ds(mine[r] * STRIPS, STRIPS)], own_sem.at[2 * r + half])
+                got[r][half].at[pl.ds(mine[r] * STRIPS, STRIPS)], own_sem.at[PARTS * r + half])
             for r in range(2)
         ])
     load_fixed = pltpu.make_async_copy(fixed_in, fixed, own_sem.at[10])
     load_table = pltpu.make_async_copy(table_in, table, own_sem.at[11])
     load_fixed.start()
     load_table.start()
-    for copy in own[0] + own[1]:
-        copy.start()
+    for copies in own:
+        for copy in copies:
+            copy.start()
     for peer in peers[0]:
         pl.semaphore_signal(ready, inc=1, device_id={"slab": peer}, device_id_type=MESH)
 
@@ -265,17 +273,11 @@
     group_base = (p // group_rows) * group_rows
     tile_ring = [lax.rem(q + i, tiles) for i in range(tiles)]
 
+    row_ring = [lax.rem(p + j, group_rows) for j in range(group_rows)]
+
     def to_group(send):
-        for i in range(1, tiles):
-            send(member - q + tile_ring[i], (p, tile_ring[i]))
-
-        def row(j, carry):
-            at = lax.rem(p + j, group_rows)
-            for i in range(tiles):
-                send(at * tiles + tile_ring[i], (group_base + at, tile_ring[i]))
-            return carry
-
-        lax.fori_loop(1, group_rows, row, 0)
+        for j, i in shuffled(group_rows, tiles):
+            send(row_ring[j] * tiles + tile_ring[i], (group_base + row_ring[j], tile_ring[i]))
 
     def send_label(peer, device):
         pltpu.make_async_remote_copy(
@@ -325,6 +327,10 @@
 
     to_scalars.wait()
 
+    turns = sorted(
+        ((r, i) for r in range(2) for i in range(len(peers[r]))),
+        key=lambda turn: (turn[1] / len(peers[turn[0]]), turn[0]))
+
     def second(half):
         for r in (1, 0):
             own[half][r].wait()
@@ -336,14 +342,14 @@
                 partner[r, s, place, :] = got[r][half][inv_s[r, 0, mine[r] * STRIPS + s]]
                 for peer in peers[r]:
                     pick[r][half, s, peer] = got[r][half][inv_s[r, 0, peer * STRIPS + s]]
-            for r in (0, 1):
+            for r, i in turns:
                 place = chunk_rows(r, mine[r], half)
-                for peer in peers[r]:
-                    pltpu.make_async_remote_copy(
-                        src_ref=pick[r].at[half, s, peer], dst_ref=partner.at[r, s, place, :],
-                        send_sem=send_sem.at[5 + r], recv_sem=slot_sem.at[r, s],
-                        device_id={axes[r]: peer}, device_id_type=MESH,
-                    ).start()
+                peer = peers[r][i]
+                pltpu.make_async_remote_copy(
+                    src_ref=pick[r].at[half, s, peer], dst_ref=partner.at[r, s, place, :],
+                    send_sem=send_sem.at[5 + r], recv_sem=slot_sem.at[r, s],
+                    device_id={axes[r]: peer}, device_id_type=MESH,
+                ).start()
             return carry
 
         lax.fori_loop(0, STRIPS, choose, 0)
@@ -351,7 +357,8 @@
     second(0)
     build_slot(2)
     build_slot(3)
-    second(1)
+    for half in range(1, PARTS):
+        second(half)
 
     low_half = lane8 < HALF_LANES
 
@@ -397,7 +404,16 @@
     peaks[...] = found
 
     big = 1024
+    plane_rows = RING * tiles * OWNED
     low_rows = lax.broadcasted_iota(jnp.int32, (GROUP * SHARE, W), 1) < HALF_LANES
+
+    def send_owner(op, oq):
+        pltpu.make_async_remote_copy(
+            src_ref=packed.at[op * tiles + oq], dst_ref=owned.at[me],
+            send_sem=send_sem.at[8], recv_sem=owner_sem,
+            device_id=(op, oq), device_id_type=MESH,
+        ).start()
+
     for s in range(STRIPS):
         local_wait(rows_got.at[s, pl.ds(0, GROUP - 1)], rows_sem.at[s])
         rows_here = rows_got[s].reshape(GROUP * SHARE, W)
@@ -407,40 +423,25 @@
             jnp.where(low_rows, high, pltpu.roll(low, HALF_LANES, 1)),
             jnp.where(low_rows, pltpu.roll(high, HALF_LANES, 1), low),
         ], 0).astype(BF16)
-
-        def add(i, carry):
-            at = pl.ds(pl.multiple_of(i * big, big), big)
-            total = dot(onehot[s, at, :], both)
-            if s > 0:
-                total = total + sums[at, :]
-            if s < STRIPS - 1:
-                sums[at, :] = total
-            else:
-                total = (total + pltpu.roll(total, HALF_LANES, 1)).reshape(big // OWNED, 2, 8, W)
-                owners = pl.ds(i * (big // OWNED), big // OWNED)
-                packed[owners] = jnp.where(low_half[None], total[:, 0], total[:, 1])
-            return carry
-
-        lax.fori_loop(0, devices * OWNED // big, add, 0)
-
-    def send_owner(op, oq):
-        pltpu.make_async_remote_copy(
-            src_ref=packed.at[op * tiles + oq], dst_ref=owned.at[me],
-            send_sem=send_sem.at[8], recv_sem=owner_sem,
-            device_id=(op, oq), device_id_type=MESH,
-        ).start()
-
-    def owner_row(j, carry):
-        op = lax.rem(z + 2 + j // RING, RING) * RING + lax.rem(x + 2 + lax.rem(j, RING), RING)
-        for oq in peers[1] + [q]:
-            send_owner(op, oq)
-        return carry
-
-    own_row = 2 * RING + 2
-    lax.fori_loop(0, own_row, owner_row, 0)
-    for oq in peers[1]:
-        send_owner(p, oq)
-    lax.fori_loop(own_row + 1, slabs, owner_row, 0)
+        if s < STRIPS - 1:
+            def add(i, carry):
+                at = pl.ds(pl.multiple_of(i * big, big), big)
+                total = dot(onehot[s, at, :], both)
+                sums[at, :] = total if s == 0 else total + sums[at, :]
+                return carry
+
+            lax.fori_loop(0, devices * OWNED // big, add, 0)
+        else:
+            for i in range(RING):
+                oz = lax.rem(z + 2 + i, RING)
+                at = pl.ds(pl.multiple_of(oz * plane_rows, plane_rows), plane_rows)
+                total = dot(onehot[s, at, :], both) + sums[at, :]
+                total = (total + pltpu.roll(total, HALF_LANES, 1)).reshape(RING * tiles, 2, 8, W)
+                packed[pl.ds(oz * RING * tiles, RING * tiles)] = jnp.where(
+                    low_half[None], total[:, 0], total[:, 1])
+                for dx, dq in shuffled(RING, tiles, i != 2):
+                    send_owner(oz * RING + lax.rem(x + dx, RING), tile_ring[dq])
+
     last = pltpu.make_async_copy(packed.at[me], owned.at[me], own_sem.at[4])
     last.start()
 
@@ -487,12 +488,10 @@
         + [
             pltpu.VMEM((STRIPS, H, W), F32),
             pltpu.VMEM((2, TABLE_ROWS, HALF), BF16),
-            pltpu.VMEM((slabs * STRIPS, H // slabs // 2, W), F32),
-            pltpu.VMEM((slabs * STRIPS, H // slabs // 2, W), F32),
-            pltpu.VMEM((tiles * STRIPS, H // tiles // 2, W), F32),
-            pltpu.VMEM((tiles * STRIPS, H // tiles // 2, W), F32),
-            pltpu.VMEM((2, STRIPS, slabs, H // slabs // 2, W), F32),
-            pltpu.VMEM((2, STRIPS, tiles, H // tiles // 2, W), F32),
+            [pltpu.VMEM((slabs * STRIPS, H // slabs // PARTS, W), F32)] * PARTS
+            + [pltpu.VMEM((tiles * STRIPS, H // tiles // PARTS, W), F32)] * PARTS,
+            pltpu.VMEM((PARTS, STRIPS, slabs, H // slabs // PARTS, W), F32),
+            pltpu.VMEM((PARTS, STRIPS, tiles, H // tiles // PARTS, W), F32),
             pltpu.VMEM((2, STRIPS, H, W), F32),
             pltpu.VMEM((slabs, 8, W), jnp.int32),
             pltpu.VMEM((tiles, 8, W), jnp.int32),
@@ -506,7 +505,7 @@
             pltpu.VMEM((STRIPS, devices * OWNED, GROUP * PIECES), BF16),
             pltpu.VMEM((devices * OWNED, W), F32),
             pltpu.VMEM((devices, 8, W), F32),
-            dma((9,)), dma((2, 2)), dma((2,)), dma, dma((2, STRIPS)), dma((STRIPS,)), dma((12,)), dma,
+            dma((9,)), dma((2, PARTS)), dma((2,)), dma, dma((2, STRIPS)), dma((STRIPS,)), dma((12,)), dma,
             pltpu.SemaphoreType.REGULAR,
         ],
         compiler_params=pltpu.CompilerParams(

time: 73.4 us -> 71.3 us (0.971)
  Pallas kernels: 72 us -> 69.9 us
    pallas_call x1, Pallas kernels: 69.9 us -> 67.9 us  [local(): pl.pallas_call(functools.partial(whole_kernel, slabs, tiles), out_shape=(...]
where the time goes in v5:
time: 71.3 us; the launch traced here: 71.2 us
  Pallas kernels  69.9 us (98%)
  between operations  1.29 us (2%)
    pallas_call x1, Pallas kernels, local(): pl.pallas_call(functools.partial(whole_kernel, slabs, tiles), out_shape=(...  67.9 us
    pallas_call x1, Pallas kernels, local(): pl.pallas_call(finish_kernel, out_shape=(jax.ShapeDtypeStruct((2, STRIPS)...  2.02 us

profile of v5, /device:TPU:1, one launch (start us, length us, event | category | flops | bytes accessed | tf_op | source)
XLA Modules:
  0.0 71.2 jit_solution(13222203488937211770)
XLA Ops:
  1.3 67.9 %register_merge.1 = (f32[8,128]{1,0:T(8,128)}, f32[128,8,128]{2,1,0:T(8,128)}) custom-call(s32[2,4]{1,0:T(2,128)} %dest_in.1, s32[2,4]{1,0:T(2,128)} %slot_in.1, s32[2,2,4]{2,1,0:T(2,128)} %shifts_in.1, s32[1]{0:T(128)S(6)} %copy.10.live, s32[64]{0:T(128)} %block_in.1, f32[2,4,512,128]{3,2,1,0:T(8,128)} %moving.1, f32[4,512,128]{2,1,0:T(8,128)} %fixed_in.1, ...), custom_call_target="tpu_custom_call" | custom-call | tf_op jit(solution)/shard_map/register_merge/pallas_call | solution.py:479
  69.1 2.0 %finish_blocks.1 = (f32[2,4]{1,0:T(2,128)}, f32[16,32,128]{2,1,0:T(8,128)}) custom-call(f32[8,128]{1,0:T(8,128)} %get-tuple-element.4.found, f32[128,8,128]{2,1,0:T(8,128)} %get-tuple-element.5.owned), custom_call_target="tpu_custom_call" | custom-call | tf_op jit(solution)/shard_map/finish_blocks/pallas_call | solution.py:516

commit v6 on v5

--- a/solution.py
+++ b/solution.py
@@ -442,8 +442,7 @@
                 for dx, dq in shuffled(RING, tiles, i != 2):
                     send_owner(oz * RING + lax.rem(x + dx, RING), tile_ring[dq])
 
-    last = pltpu.make_async_copy(packed.at[me], owned.at[me], own_sem.at[4])
-    last.start()
+    owned[me] = packed[me]
 
     for r in range(2):
         local_wait(code[r].at[pl.ds(0, sizes[r] - 1)], send_sem.at[r])
@@ -452,7 +451,6 @@
     local_wait(label_got.at[pl.ds(0, GROUP - 1)], send_sem.at[4])
     local_wait(spread.at[:, pl.ds(0, GROUP - 1)], send_sem.at[7])
 
-    last.wait()
     local_wait(packed.at[pl.ds(0, devices - 1)], owner_sem)
     local_wait(packed.at[pl.ds(0, devices - 1)], send_sem.at[8])
 
@@ -483,7 +481,7 @@
             jax.ShapeDtypeStruct((devices, 8, W), F32),
         ),
         in_specs=[anywhere] * 3 + [pl.BlockSpec(memory_space=pltpu.SMEM)] + [anywhere] * 4,
-        out_specs=(vmem, anywhere),
+        out_specs=(vmem, vmem),
         scratch_shapes=[pltpu.SMEM(a.shape, jnp.int32) for a in small if a.shape != (1,)]
         + [
             pltpu.VMEM((STRIPS, H, W), F32),

time: 71.3 us -> 71.4 us (level)
  no operation moved by 1% of the time
where the time goes in v6:
time: 71.4 us; the launch traced here: 71.3 us
  Pallas kernels  70 us (98%)
  between operations  1.29 us (2%)
    pallas_call x1, Pallas kernels, local(): pl.pallas_call(functools.partial(whole_kernel, slabs, tiles), out_shape=(...  68 us
    pallas_call x1, Pallas kernels, local(): pl.pallas_call(finish_kernel, out_shape=(jax.ShapeDtypeStruct((2, STRIPS)...  2.02 us

profile of v6, /device:TPU:1, one launch (start us, length us, event | category | flops | bytes accessed | tf_op | source)
XLA Modules:
  0.0 71.3 jit_solution(8067029445134652582)
XLA Ops:
  1.3 68.0 %register_merge.1 = (f32[8,128]{1,0:T(8,128)}, f32[128,8,128]{2,1,0:T(8,128)}) custom-call(s32[2,4]{1,0:T(2,128)} %dest_in.1, s32[2,4]{1,0:T(2,128)} %slot_in.1, s32[2,2,4]{2,1,0:T(2,128)} %shifts_in.1, s32[1]{0:T(128)S(6)} %copy.10.live, s32[64]{0:T(128)} %block_in.1, f32[2,4,512,128]{3,2,1,0:T(8,128)} %moving.1, f32[4,512,128]{2,1,0:T(8,128)} %fixed_in.1, ...), custom_call_target="tpu_custom_call" | custom-call | tf_op jit(solution)/shard_map/register_merge/pallas_call | solution.py:477
  69.2 2.0 %finish_blocks.1 = (f32[2,4]{1,0:T(2,128)}, f32[16,32,128]{2,1,0:T(8,128)}) custom-call(f32[8,128]{1,0:T(8,128)} %get-tuple-element.4.found, f32[128,8,128]{2,1,0:T(8,128)} %get-tuple-element.5.owned), custom_call_target="tpu_custom_call" | custom-call | tf_op jit(solution)/shard_map/finish_blocks/pallas_call | solution.py:514
